TPU v7x, 256 devices: a 8x8x2 block of a 8x8x16 slice. The times are simulated.
256 devices in a mesh: rep: 2 (over z), gx: 128 (over y, x, core).
Axes of the slice: x: 8, y: 8, z: 2, core: 2. Of those that a mesh axis runs over, the one named last changes fastest.
The devices are a block of a 8x8x16 slice.
Arguments:
- positions: float32 [3, 1048576], P(None, ('rep', 'gx')), parts along dimension 1, may hold values from 0 to 512, as said below
- polar: float32 [1048576], P(('rep', 'gx')), parts along dimension 0, may hold values from 0.25 to 1
- field_ext: float32 [3, 1048576], P(None, ('rep', 'gx')), parts along dimension 1, may hold values from -10 to 10
- tile_atom: int32 [1048576], P(('rep', 'gx')), parts along dimension 0, may hold values from 0 to 4095, as said below
- tile_list: int32 [8192, 3], P(('rep', 'gx')), parts along dimension 0, may hold values from 0 to 63, as said below
- image_shift: int32 [2, 8192, 3], P(None, ('rep', 'gx')), parts along dimension 1, may hold values from 0 to 1, as said below
Outputs:
- dipoles: float32 [3, 1048576], P(None, ('rep', 'gx')), parts along dimension 1
- residual: float32 [3, 1048576], P(None, ('rep', 'gx')), parts along dimension 1
There are 2 independent parts, one for each index of `rep`. A program takes and returns all parts, laid end to end along the dimension named above; each array names one. Nothing has to cross between parts.
Inputs may be any that keep to these rules, and one draw needn't show every extreme that they name: `positions`: coordinates lie in a box of 512 by 128 by 64; the atoms of slab s have first coordinate between 4 s and 4 s + 4; no two atoms, and no atom and a periodic image of another, are closer than 1.4. `tile_atom`: for each slab, a permutation of 0 to 4095. `tile_list`: entry 0 of a tile is the tile's own index within its slab. Entry n of a tile of slab s names tile n of slab s if n < 32, else tile n - 32 of slab s + 1 (slab 0 after the last). `image_shift`: offsets along the second and third coordinates in box lengths, one pair for each entry of tile_list; zero for entry 0.
All inputs are finite; a program needn't handle non-finite values.
Results may differ from a plain program's by a relative error of at most 0.0003.
Values sent between devices are 32-bit elements; how exact they have to be, the bound alone decides.
A program may use at most 64 MiB of HBM per device.

v0:
```python
import functools
import math

import jax
import jax.numpy as jnp
from jax import lax
from jax.sharding import Mesh
from jax.sharding import PartitionSpec as P

ITERS = 4
GX = ("gx_0", "gx_1", "gx_2")
REP_GX = ("rep", "gx_0", "gx_1", "gx_2")


thole_factor = 0.39


def over_axes(shard, axes):
    return functools.reduce(lax.psum, axes, shard)


def passed_along(value, axis, steps):
    count = lax.axis_size(axis)
    pairs = [(source, (source + steps) % count) for source in range(count)]
    return lax.ppermute(value, axis, pairs)


def pair_block(
    place_left, root_left, moment_left, place_right, root_right, moment_right, weights, self_flags
):
    offset_x = place_right[:, 0, None, :] - place_left[:, 0, :, None]
    offset_y = place_right[:, 1, None, :] - place_left[:, 1, :, None]
    offset_z = place_right[:, 2, None, :] - place_left[:, 2, :, None]
    dist_sq = offset_x * offset_x + offset_y * offset_y + offset_z * offset_z
    tile_width = place_left.shape[2]
    row_ids = lax.broadcasted_iota(jnp.int32, (tile_width, tile_width), 0)
    column_ids = lax.broadcasted_iota(jnp.int32, (tile_width, tile_width), 1)
    same_atom = jnp.logical_and(self_flags[:, None, None] > 0, (row_ids == column_ids)[None])
    dist_sq = jnp.where(same_atom, 1.0, dist_sq)
    inv_dist = lax.rsqrt(dist_sq)
    distance = dist_sq * inv_dist
    damp_arg = thole_factor * dist_sq * distance / (root_left[:, :, None] * root_right[:, None, :])
    decay = jnp.exp(-damp_arg)
    inv_cube = jnp.where(same_atom, 0.0, weights[:, None, None] * inv_dist * inv_dist * inv_dist)
    coeff_three = (1.0 - decay) * inv_cube
    coeff_five = 3.0 * (1.0 - (1.0 + damp_arg) * decay) * inv_cube * inv_dist * inv_dist
    offsets = (offset_x, offset_y, offset_z)
    proj_right = (
        offset_x * moment_right[:, 0, None, :]
        + offset_y * moment_right[:, 1, None, :]
        + offset_z * moment_right[:, 2, None, :]
    )
    proj_left = (
        offset_x * moment_left[:, 0, :, None]
        + offset_y * moment_left[:, 1, :, None]
        + offset_z * moment_left[:, 2, :, None]
    )
    lift_right = coeff_five * proj_right
    lift_left = coeff_five * proj_left
    field_left = jnp.stack(
        [
            jnp.sum(
                lift_right * offsets[component] - coeff_three * moment_right[:, component, None, :],
                axis=2,
            )
            for component in range(3)
        ],
        axis=1,
    )
    field_right = jnp.stack(
        [
            jnp.sum(
                lift_left * offsets[component] - coeff_three * moment_left[:, component, :, None],
                axis=1,
            )
            for component in range(3)
        ],
        axis=1,
    )
    return (field_left, field_right)


def slab_fields(
    window_place,
    window_root,
    window_moment,
    left_index,
    right_index,
    image_vec,
    weights,
    self_flags,
):
    entries = left_index.shape[0]
    block_size = math.gcd(entries, 32)
    window_size = window_place.shape[0]
    tile_width = window_place.shape[2]
    slot_ids = jnp.arange(window_size, dtype=jnp.int32)

    def accumulate(summed, first_entry):
        left_rows = lax.dynamic_slice_in_dim(left_index, first_entry, block_size)
        right_rows = lax.dynamic_slice_in_dim(right_index, first_entry, block_size)
        image_rows = lax.dynamic_slice_in_dim(image_vec, first_entry, block_size)
        weight_rows = lax.dynamic_slice_in_dim(weights, first_entry, block_size)
        flag_rows = lax.dynamic_slice_in_dim(self_flags, first_entry, block_size)
        place_left = jnp.take(window_place, left_rows, axis=0)
        place_right = jnp.take(window_place, right_rows, axis=0) + image_rows[:, :, None]
        field_left, field_right = pair_block(
            place_left,
            jnp.take(window_root, left_rows, axis=0),
            jnp.take(window_moment, left_rows, axis=0),
            place_right,
            jnp.take(window_root, right_rows, axis=0),
            jnp.take(window_moment, right_rows, axis=0),
            weight_rows,
            flag_rows,
        )
        hit_left = (left_rows[:, None] == slot_ids[None, :]).astype(jnp.float32)
        hit_right = (right_rows[:, None] == slot_ids[None, :]).astype(jnp.float32)
        summed = summed + jnp.einsum(
            "ew,ef->wf",
            hit_left,
            field_left.reshape(block_size, 3 * tile_width),
            precision=lax.Precision.HIGHEST,
        )
        summed = summed + jnp.einsum(
            "ew,ef->wf",
            hit_right,
            field_right.reshape(block_size, 3 * tile_width),
            precision=lax.Precision.HIGHEST,
        )
        return (summed, None)

    first_entries = jnp.arange(0, entries, block_size, dtype=jnp.int32)
    summed, _ = lax.scan(
        accumulate, jnp.zeros((window_size, 3 * tile_width), jnp.float32), first_entries
    )
    return summed.reshape(window_size, 3, tile_width)


def image_vectors(lists, shifts, last_flag, tile_count, box_x, box_y, box_z):
    crossing = lists >= tile_count
    wrapped = jnp.where(jnp.logical_and(crossing, last_flag), box_x, 0.0)
    vectors = jnp.stack(
        [wrapped, shifts[0].astype(jnp.float32) * box_y, shifts[1].astype(jnp.float32) * box_z],
        axis=-1,
    )
    return vectors.reshape(-1, 3)


def two_products(vector, applied):
    return (over_axes(jnp.sum(vector * vector), GX), over_axes(jnp.sum(vector * applied), GX))


def on_device(positions, polar, field_ext, tile_atom, tile_list, image_shift):
    tile_count = tile_list.shape[0]
    links = tile_list.shape[1]
    atom_count = tile_atom.shape[0]
    tile_width = atom_count // tile_count
    slab_count = lax.axis_size(GX)
    position_id = lax.axis_index(GX)
    tiled_place = positions[:, tile_atom].reshape(3, tile_count, tile_width).transpose(1, 0, 2)
    tiled_polar = polar[tile_atom].reshape(tile_count, tile_width)
    tiled_root = jnp.sqrt(tiled_polar)
    tiled_rhs = field_ext[:, tile_atom].reshape(3, tile_count, tile_width).transpose(1, 0, 2)
    packed = jnp.concatenate([tiled_place, tiled_root[:, None, :]], axis=1)
    box_x = 4.0 * slab_count
    box_y = 128.0
    box_z = 2.0 * tile_count
    entry_ids = jnp.arange(links, dtype=jnp.int32)
    own_left = jnp.repeat(jnp.arange(tile_count, dtype=jnp.int32), links)
    own_right = tile_list.reshape(-1)
    own_weights = jnp.tile(jnp.where(entry_ids == 0, 0.5, 1.0), tile_count)
    own_self = jnp.tile((entry_ids == 0).astype(jnp.int32), tile_count)
    own_image = image_vectors(
        tile_list, image_shift, position_id == slab_count - 1, tile_count, box_x, box_y, box_z
    )
    ahead = passed_along(packed, GX, -1)
    window_pack = jnp.concatenate([packed, ahead], axis=0)

    def operate(direction):
        ahead_moment = passed_along(direction, GX, -1)
        summed = slab_fields(
            window_pack[:, :3],
            window_pack[:, 3],
            jnp.concatenate([direction, ahead_moment], axis=0),
            own_left,
            own_right,
            own_image,
            own_weights,
            own_self,
        )
        returned = passed_along(summed[tile_count:], GX, 1)
        return direction / tiled_polar[:, None, :] - (summed[:tile_count] + returned)

    solution = jnp.zeros_like(tiled_rhs)
    resid = tiled_rhs
    applied = operate(resid)
    norm_now, product = two_products(resid, applied)
    step_size = norm_now / product
    direction, along = (resid, applied)
    for iteration in range(ITERS):
        solution = solution + step_size * direction
        resid = resid - step_size * along
        if iteration + 1 < ITERS:
            applied = operate(resid)
            norm_next, product = two_products(resid, applied)
            ratio = norm_next / norm_now
            step_size = norm_next / (product - ratio * norm_next / step_size)
            direction = resid + ratio * direction
            along = applied + ratio * along
            norm_now = norm_next
    dipoles = (
        jnp.zeros((3, atom_count), jnp.float32)
        .at[:, tile_atom]
        .set(solution.transpose(1, 0, 2).reshape(3, atom_count))
    )
    residual = (
        jnp.zeros((3, atom_count), jnp.float32)
        .at[:, tile_atom]
        .set(resid.transpose(1, 0, 2).reshape(3, atom_count))
    )
    return (dipoles, residual)


def solution(mesh):
    split = Mesh(mesh.devices.reshape(mesh.shape["rep"], 8, 8, 2), ("rep", "gx_0", "gx_1", "gx_2"))
    return jax.shard_map(
        on_device,
        mesh=split,
        in_specs=(
            P(None, REP_GX),
            P(REP_GX),
            P(None, REP_GX),
            P(REP_GX),
            P(REP_GX, None),
            P(None, REP_GX, None),
        ),
        out_specs=(P(None, REP_GX), P(None, REP_GX)),
        check_vma=False,
    )
```

profile of v0, /device:TPU:513, one launch (start us, length us, event | category | flops | bytes accessed | tf_op | source)
XLA Modules:
  0.0 492.2 jit_solution(17890280772441615265)
XLA Ops:
  1.4 23.0 %gather_fusion.25 = f32[4096]{0:T(1024)S(1)} fusion(f32[4096]{0:T(1024)S(1)} %copy-done, s32[4096]{0:T(1024)S(1)} %get-tuple-element.975), kind=kCustom, calls=%fused_computation.25 | custom fusion | bytes 49152 | tf_op jit(solution)/shard_map/gather | solution.py:162
  25.1 14.1 %gather_fusion.26 = f32[4096,3]{1,0:T(8,128)} fusion(f32[3,4096]{0,1:T(8,128)S(1)} %copy.89, s32[4096]{0:T(1024)S(1)} %get-tuple-element.975), kind=kCustom, calls=%fused_computation.26 | custom fusion | bytes 114688 | tf_op jit(solution)/shard_map/gather | solution.py:161
  41.4 20.5 %collective-permute-start = (f32[32,4,128]{2,0,1:T(8,128)S(1)}, f32[32,4,128]{2,0,1:T(8,128)S(1)}, u32[]{:S(2)}, u32[]{:S(2)}) collective-permute-start(f32[32,4,128]{2,0,1:T(8,128)S(1)} %pad_maximum_fusion.5), channel_id=1, source_target_pairs={{0,127},{1,0},{2,1},{3,2},{4,3},{5,4},{6,5},{7,6},{8,7},{9,8},{10,... | collective-permute-start | bytes 196616 | tf_op jit(solution)/shard_map/ppermute | solution.py:25
  62.6 14.1 %gather_fusion.24 = f32[4096,3]{1,0:T(8,128)} fusion(f32[3,4096]{0,1:T(8,128)S(1)} %copy.86, s32[4096]{0:T(1024)S(1)} %get-tuple-element.975), kind=kCustom, calls=%fused_computation.24 | custom fusion | bytes 114688 | tf_op jit(solution)/shard_map/gather | solution.py:164
  82.9 46.8 %while.48 = (s32[]{:T(128)}, f32[64,384]{1,0:T(8,128)S(1)}, s32[3]{0:T(128)S(1)}, s32[96]{0:T(128)S(1)}, s32[96]{0:T(128)S(1)}, /*index=5*/s32[96]{0:T(128)S(1)}...) while((s32[]{:T(128)}, f32[64,384]{1,0:T(8,128)S(1)}, ...), condition=%wide.region_11.14_spmd.clone.clone, body=%wide.region_4.13_spmd.clone.clone.sunk | while | flops 53144164 | bytes 2176077 | solution.py:134
  90.0 7.8 %fusion.181 = (f32[32,128]{1,0:T(8,128)S(1)}, f32[32,128]{1,0:T(8,128)S(1)}, f32[32,128]{1,0:T(8,128)S(1)}, f32[32,128]{1,0:T(8,128)S(1)}, f32[32,128]{1,0:T(8,128)S(1)}, /*index=5*/f32[32,128]{1,0:T(8,128)S(1)}) fusion(f32[32,128]{1,0:T(8,128)S(1)} %bitcast.385, f32[32,128]{1,0:T(8,128)S(1)} %bitcast.397, f32[32,128]{1,0:T(8,128)S(1)} %bitcast.361, ...), kind=kLoop, calls=%fused_computation.66.clone.1 | loop fusion | flops 34054144 | bytes 344224 | tf_op jit(solution)/shard_map/while/body/eval_jaxpr/reduce_sum | solution.py:72
  105.6 7.8 %fusion.181 = (f32[32,128]{1,0:T(8,128)S(1)}, f32[32,128]{1,0:T(8,128)S(1)}, f32[32,128]{1,0:T(8,128)S(1)}, f32[32,128]{1,0:T(8,128)S(1)}, f32[32,128]{1,0:T(8,128)S(1)}, /*index=5*/f32[32,128]{1,0:T(8,128)S(1)}) fusion(f32[32,128]{1,0:T(8,128)S(1)} %bitcast.385, f32[32,128]{1,0:T(8,128)S(1)} %bitcast.397, f32[32,128]{1,0:T(8,128)S(1)} %bitcast.361, ...), kind=kLoop, calls=%fused_computation.66.clone.1 | loop fusion | flops 34054144 | bytes 344224 | tf_op jit(solution)/shard_map/while/body/eval_jaxpr/reduce_sum | solution.py:72
  131.9 11.4 %all-reduce.7 = (f32[]{:T(128)}, f32[]{:T(128)}) all-reduce(f32[]{:T(128)} %get-tuple-element.759, f32[]{:T(128)} %get-tuple-element.758), channel_id=1, replica_groups=mesh['rep'=2,'gx_0'=8,'gx_1'=8,'gx_2'=2] {'gx_0'}, use_global_device_ids=true, to_apply=%region_1.2 | all-reduce | flops 2 | bytes 16 | tf_op jit(solution)/shard_map/psum | solution.py:19
  143.2 14.6 %all-reduce.3 = (f32[]{:T(128)}, f32[]{:T(128)}) all-reduce(f32[]{:T(128)} %get-tuple-element.862, f32[]{:T(128)} %get-tuple-element.863), channel_id=1, replica_groups=mesh['rep'=2,'gx_0'=8,'gx_1'=8,'gx_2'=2] {'gx_1'}, use_global_device_ids=true, to_apply=%region_2.3 | all-reduce | flops 2 | bytes 16 | tf_op jit(solution)/shard_map/psum | solution.py:19
  157.9 10.4 %all-reduce.11 = (f32[]{:T(128)}, f32[]{:T(128)}) all-reduce(f32[]{:T(128)} %get-tuple-element.854, f32[]{:T(128)} %get-tuple-element.855), channel_id=1, replica_groups=mesh['rep'=2,'gx_0'=8,'gx_1'=8,'gx_2'=2] {'gx_2'}, use_global_device_ids=true, to_apply=%region_3.4 | all-reduce | flops 2 | bytes 16 | tf_op jit(solution)/shard_map/psum | solution.py:19
  173.7 47.5 %while.49 = (s32[]{:T(128)}, f32[64,384]{1,0:T(8,128)S(1)}, s32[3]{0:T(128)S(1)}, s32[96]{0:T(128)S(1)}, s32[96]{0:T(128)S(1)}, /*index=5*/s32[96]{0:T(128)S(1)}...) while((s32[]{:T(128)}, f32[64,384]{1,0:T(8,128)S(1)}, ...), condition=%wide.region_27.30_spmd.clone.clone, body=%wide.region_20.29_spmd.clone.clone.sunk | while | flops 53144164 | bytes 2176077 | solution.py:134
  224.4 12.2 %all-reduce.6 = (f32[]{:T(128)}, f32[]{:T(128)}) all-reduce(f32[]{:T(128)} %get-tuple-element.757, f32[]{:T(128)} %get-tuple-element.756), channel_id=1, replica_groups=mesh['rep'=2,'gx_0'=8,'gx_1'=8,'gx_2'=2] {'gx_0'}, use_global_device_ids=true, to_apply=%region_17.20 | all-reduce | flops 2 | bytes 16 | tf_op jit(solution)/shard_map/psum | solution.py:19
  236.5 16.3 %all-reduce.2 = (f32[]{:T(128)}, f32[]{:T(128)}) all-reduce(f32[]{:T(128)} %get-tuple-element.860, f32[]{:T(128)} %get-tuple-element.861), channel_id=1, replica_groups=mesh['rep'=2,'gx_0'=8,'gx_1'=8,'gx_2'=2] {'gx_1'}, use_global_device_ids=true, to_apply=%region_18.21 | all-reduce | flops 2 | bytes 16 | tf_op jit(solution)/shard_map/psum | solution.py:19
  252.8 10.5 %all-reduce.10 = (f32[]{:T(128)}, f32[]{:T(128)}) all-reduce(f32[]{:T(128)} %get-tuple-element.852, f32[]{:T(128)} %get-tuple-element.853), channel_id=1, replica_groups=mesh['rep'=2,'gx_0'=8,'gx_1'=8,'gx_2'=2] {'gx_2'}, use_global_device_ids=true, to_apply=%region_19.22 | all-reduce | flops 2 | bytes 16 | tf_op jit(solution)/shard_map/psum | solution.py:19
  272.1 46.8 %while.50 = (s32[]{:T(128)}, f32[64,384]{1,0:T(8,128)S(1)}, s32[3]{0:T(128)S(1)}, s32[96]{0:T(128)S(1)}, s32[96]{0:T(128)S(1)}, /*index=5*/s32[96]{0:T(128)S(1)}...) while((s32[]{:T(128)}, f32[64,384]{1,0:T(8,128)S(1)}, ...), condition=%wide.region_43.46_spmd.clone.clone, body=%wide.region_36.45_spmd.clone.clone.sunk | while | flops 53144164 | bytes 2176077 | solution.py:134
  322.0 12.1 %all-reduce.5 = (f32[]{:T(128)}, f32[]{:T(128)}) all-reduce(f32[]{:T(128)} %get-tuple-element.755, f32[]{:T(128)} %get-tuple-element.754), channel_id=1, replica_groups=mesh['rep'=2,'gx_0'=8,'gx_1'=8,'gx_2'=2] {'gx_0'}, use_global_device_ids=true, to_apply=%region_33.36 | all-reduce | flops 2 | bytes 16 | tf_op jit(solution)/shard_map/psum | solution.py:19
  334.1 16.2 %all-reduce.1 = (f32[]{:T(128)}, f32[]{:T(128)}) all-reduce(f32[]{:T(128)} %get-tuple-element.858, f32[]{:T(128)} %get-tuple-element.859), channel_id=1, replica_groups=mesh['rep'=2,'gx_0'=8,'gx_1'=8,'gx_2'=2] {'gx_1'}, use_global_device_ids=true, to_apply=%region_34.37 | all-reduce | flops 2 | bytes 16 | tf_op jit(solution)/shard_map/psum | solution.py:19
  350.3 10.4 %all-reduce.9 = (f32[]{:T(128)}, f32[]{:T(128)}) all-reduce(f32[]{:T(128)} %get-tuple-element.850, f32[]{:T(128)} %get-tuple-element.851), channel_id=1, replica_groups=mesh['rep'=2,'gx_0'=8,'gx_1'=8,'gx_2'=2] {'gx_2'}, use_global_device_ids=true, to_apply=%region_35.38 | all-reduce | flops 2 | bytes 16 | tf_op jit(solution)/shard_map/psum | solution.py:19
  368.9 47.5 %while.51 = (s32[]{:T(128)}, f32[64,384]{1,0:T(8,128)S(1)}, s32[3]{0:T(128)S(1)}, s32[96]{0:T(128)S(1)}, s32[96]{0:T(128)S(1)}, /*index=5*/s32[96]{0:T(128)S(1)}...) while((s32[]{:T(128)}, f32[64,384]{1,0:T(8,128)S(1)}, ...), condition=%wide.region_59.62_spmd.clone.clone, body=%wide.region_52.61_spmd.clone.clone.sunk | while | flops 53144164 | bytes 2176077 | solution.py:134
  419.5 12.2 %all-reduce.4 = (f32[]{:T(128)}, f32[]{:T(128)}) all-reduce(f32[]{:T(128)} %get-tuple-element.753, f32[]{:T(128)} %get-tuple-element.752), channel_id=1, replica_groups=mesh['rep'=2,'gx_0'=8,'gx_1'=8,'gx_2'=2] {'gx_0'}, use_global_device_ids=true, to_apply=%region_49.52 | all-reduce | flops 2 | bytes 16 | tf_op jit(solution)/shard_map/psum | solution.py:19
  431.6 16.2 %all-reduce = (f32[]{:T(128)}, f32[]{:T(128)}) all-reduce(f32[]{:T(128)} %get-tuple-element.856, f32[]{:T(128)} %get-tuple-element.857), channel_id=1, replica_groups=mesh['rep'=2,'gx_0'=8,'gx_1'=8,'gx_2'=2] {'gx_1'}, use_global_device_ids=true, to_apply=%region_50.53 | all-reduce | flops 2 | bytes 16 | tf_op jit(solution)/shard_map/psum | solution.py:19
  447.9 10.5 %all-reduce.8 = (f32[]{:T(128)}, f32[]{:T(128)}) all-reduce(f32[]{:T(128)} %get-tuple-element.848, f32[]{:T(128)} %get-tuple-element.849), channel_id=1, replica_groups=mesh['rep'=2,'gx_0'=8,'gx_1'=8,'gx_2'=2] {'gx_2'}, use_global_device_ids=true, to_apply=%region_51.54 | all-reduce | flops 2 | bytes 16 | tf_op jit(solution)/shard_map/psum | solution.py:19
  464.6 11.6 %scatter_custom_fusion.1 = f32[3,4096]{0,1:T(8,128)S(1)} fusion(s32[4096]{0:T(1024)S(1)} %get-tuple-element.976, f32[4096,3]{1,0:T(8,128)} %copy.101, f32[]{:T(128)} %constant.22.clone.1), kind=kCustom, calls=%fused_computation.317 | custom fusion | bytes 49664 | tf_op jit(solution)/shard_map/scatter | solution.py:220
  479.5 11.4 %scatter_custom_fusion = f32[3,4096]{0,1:T(8,128)S(1)} fusion(s32[4096]{0:T(1024)S(1)} %get-tuple-element.976, f32[4096,3]{1,0:T(8,128)} %copy.100, f32[]{:T(128)} %constant.22.clone.1), kind=kCustom, calls=%fused_computation.319 | custom fusion | bytes 49664 | tf_op jit(solution)/shard_map/scatter | solution.py:215
  (425 shorter events, 187.9 us)
Async XLA Ops:
  0.6 0.7 copy-start
  1.4 23.1 %copy-start.1 = (f32[3,4096]{1,0:T(4,128)S(1)}, f32[3,4096]{1,0:T(4,128)}, u32[]{:S(2)}) copy-start(f32[3,4096]{1,0:T(4,128)} %param.18) | copy-start | bytes 147460
  24.5 37.5 %copy-start.2 = (f32[3,4096]{1,0:T(4,128)S(1)}, f32[3,4096]{1,0:T(4,128)}, u32[]{:S(2)}) copy-start(f32[3,4096]{1,0:T(4,128)} %param.20) | copy-start | bytes 147460
  41.4 37.6 %copy-start.3 = (s32[32,3]{0,1:T(4,128)S(1)}, s32[32,3]{0,1:T(4,128)}, u32[]{:S(2)}) copy-start(s32[32,3]{0,1:T(4,128)} %param.22) | copy-start | bytes 1156
  41.4 37.8 %copy-start.4 = (s32[2,32,3]{1,0,2:T(2,128)S(1)}, s32[2,32,3]{1,0,2:T(2,128)}, u32[]{:S(2)}) copy-start(s32[2,32,3]{1,0,2:T(2,128)} %param.23) | copy-start | bytes 2308
  41.4 41.3 %collective-permute-start = (f32[32,4,128]{2,0,1:T(8,128)S(1)}, f32[32,4,128]{2,0,1:T(8,128)S(1)}, u32[]{:S(2)}, u32[]{:S(2)}) collective-permute-start(f32[32,4,128]{2,0,1:T(8,128)S(1)} %pad_maximum_fusion.5), channel_id=1, source_target_pairs={{0,127},{1,0},{2,1},{3,2},{4,3},{5,4},{6,5},{7,6},{8,7},{9,8},{10,... | collective-permute-start | bytes 196616 | tf_op jit(solution)/shard_map/ppermute | solution.py:25
  78.9 3.8 collective-permute-start.1
  129.7 1.5 collective-permute-start.2
  169.7 4.0 collective-permute-start.3
  221.2 2.4 collective-permute-start.4
  268.0 4.0 collective-permute-start.5
  318.9 2.4 collective-permute-start.6
  364.9 4.0 collective-permute-start.7
  416.4 2.4 collective-permute-start.8
where the time goes:
time: 493 us; the launch traced here: 492 us
  blocking collectives  153 us (31%)
  local copies, waits for them, and re-layouts  143 us (29%)
  other arithmetic  104 us (21%)
  loops' own time  25.6 us (5%)
  starting transfers between devices  22.5 us (5%)
  waiting for transfers between devices  21.1 us (4%)
  between operations  15.3 us (3%)
  matrix products  7.52 us (2%)
    psum x12, blocking collectives, over_axes(): return functools.reduce(lax.psum, axes, shard)  153 us
    reduce_sum x12, other arithmetic, pair_block(): jnp.sum(lift_left * offsets[component] - coeff_three * moment_left[:, com...  93.5 us
    another operation x4, loops' own time, slab_fields(): lax.scan(accumulate, jnp.zeros((window_size, 3 * tile_width), jnp.float32...  25.6 us
    gather x1, local copies, waits for them, and re-layouts, on_device(): tiled_polar = polar[tile_atom].reshape(tile_count, tile_width)  23 us
    ppermute x9, starting transfers between devices, passed_along(): return lax.ppermute(value, axis, pairs)  22.5 us
    ppermute x9, waiting for transfers between devices, passed_along(): return lax.ppermute(value, axis, pairs)  21.1 us
    gather x1, local copies, waits for them, and re-layouts, on_device(): field_ext[:, tile_atom].reshape(3, tile_count, tile_width)  14.1 us
    gather x1, local copies, waits for them, and re-layouts, on_device(): positions[:, tile_atom].reshape(3, tile_count, tile_width)  14.1 us
  transfers between devices with their start and end apart: 9, of which 8 were waited for; matrix products, arithmetic and copies ran while one was open for 4% of the time, Pallas kernels for 0%

commit v1 on v0

v1 whole, which is shorter than its diff:
```python
import functools

import jax
import jax.numpy as jnp
from jax import lax
from jax.experimental import pallas as pl
from jax.experimental.pallas import tpu as pltpu
from jax.sharding import PartitionSpec as P

ITERS = 4
MESH = pl.DeviceIdType.MESH
THOLE = 0.39
F32 = jnp.float32
ROWS = 8


def lanes(index):
    return slice(index * 128, (index + 1) * 128)


def tiled_order_kernel(pos_ref, polar_ref, field_ref, atom_ref, pack_ref, inv_alpha_ref, rhs_ref, slot_ref):
    tiles = atom_ref.shape[0]
    atom = atom_ref[...]
    high = atom // 128
    low = atom % 128

    def pick(step, found):
        hit = high == step
        cols = pl.ds(pl.multiple_of(step * 128, 128), 128)
        rows = [pos_ref[c : c + 1, cols] for c in range(3)]
        rows += [field_ref[c : c + 1, cols] for c in range(3)]
        rows.append(polar_ref[pl.ds(step, 1), :])
        new = []
        for row, old in zip(rows, found):
            wide = jnp.broadcast_to(row, (tiles, 128))
            new.append(jnp.where(hit, jnp.take_along_axis(wide, low, axis=1), old))
        return tuple(new)

    zero = jnp.zeros((tiles, 128), F32)
    found = lax.fori_loop(0, tiles, pick, (zero,) * 7)
    for c in range(3):
        pack_ref[c * tiles : (c + 1) * tiles, :] = found[c]
        rhs_ref[c * tiles : (c + 1) * tiles, :] = found[3 + c]
    pack_ref[3 * tiles : 4 * tiles, :] = lax.rsqrt(found[6])
    inv_alpha_ref[...] = 1.0 / found[6]

    high_ids = lax.broadcasted_iota(jnp.int32, (tiles, 128), 0)
    low_ids = lax.broadcasted_iota(jnp.int32, (128, 128), 0)
    lane_ids = lax.broadcasted_iota(jnp.int32, (tiles, 128), 1).astype(F32)

    def invert(step, total):
        row = atom_ref[pl.ds(step, 1), :]
        hot_high = high_ids == row // 128
        hot_low = jnp.where(low_ids == row % 128, 1.0, 0.0).astype(jnp.bfloat16)
        left = jnp.concatenate(
            [
                jnp.where(hot_high, lax.convert_element_type(step, F32), 0.0),
                jnp.where(hot_high, lane_ids, 0.0),
            ],
            axis=0,
        ).astype(jnp.bfloat16)
        return total + lax.dot_general(
            left, hot_low, (((1,), (1,)), ((), ())), preferred_element_type=F32
        )

    total = lax.fori_loop(0, tiles, invert, jnp.zeros((2 * tiles, 128), F32))
    slot_ref[...] = (total[:tiles] * 128.0 + total[tiles:]).astype(jnp.int32)


def atom_order_kernel(x_ref, r_ref, slot_ref, dipoles_ref, residual_ref):
    tiles = slot_ref.shape[0]
    slot = slot_ref[...]
    high = slot // 128
    low = slot % 128

    def pick(step, found):
        hit = high == step
        rows = [ref[pl.ds(c * tiles + step, 1), :] for ref in (x_ref, r_ref) for c in range(3)]
        new = []
        for row, old in zip(rows, found):
            wide = jnp.broadcast_to(row, (tiles, 128))
            new.append(jnp.where(hit, jnp.take_along_axis(wide, low, axis=1), old))
        return tuple(new)

    zero = jnp.zeros((tiles, 128), F32)
    found = lax.fori_loop(0, tiles, pick, (zero,) * 6)
    for c in range(3):
        for h in range(tiles):
            dipoles_ref[c : c + 1, lanes(h)] = found[c][h : h + 1, :]
            residual_ref[c : c + 1, lanes(h)] = found[3 + c][h : h + 1, :]


def pair_tensor(left, right, diagonal):
    dx = right[0] - left[0]
    dy = right[1] - left[1]
    dz = right[2] - left[2]
    square = dx * dx + dy * dy + dz * dz
    if diagonal is not None:
        square = jnp.where(diagonal, 1.0, square)
    inv = lax.rsqrt(square)
    minus_u = square * (square * inv) * (left[3] * right[3])
    decay = jnp.exp(minus_u)
    inv_square = inv * inv
    inv_cube = inv * inv_square
    if diagonal is not None:
        inv_cube = jnp.where(diagonal, 0.0, inv_cube)
    rest = 1.0 - decay
    g3 = rest * inv_cube
    g5 = (rest + minus_u * decay) * inv_cube * (3.0 * inv_square)
    ax = g5 * dx
    ay = g5 * dy
    return (
        ax * dx - g3,
        ax * dy,
        ax * dz,
        ay * dy - g3,
        ay * dz,
        g5 * dz * dz - g3,
    )


def times(t, m):
    return (
        t[0] * m[0] + t[1] * m[1] + t[2] * m[2],
        t[1] * m[0] + t[3] * m[1] + t[4] * m[2],
        t[2] * m[0] + t[4] * m[1] + t[5] * m[2],
    )


def solve_kernel(
    group,
    inner,
    pack_ref,
    rhs_ref,
    inv_alpha_ref,
    list_ref,
    shift_ref,
    x_ref,
    r_ref,
    own_t,
    pair_t,
    part,
    cols_a,
    cols_b,
    win_p,
    win_0,
    win_1,
    win_2,
    win_3,
    top,
    ret_out,
    ret_in,
    right_rows,
    hot,
    colmat,
    gram,
    sums_1,
    sums_2,
    ring_send,
    ring_recv,
    sum_send,
    sum_recv,
):
    tiles = rhs_ref.shape[0] // 3
    me = lax.axis_index("gx")
    outer = group // inner
    row, col = me // inner, me % inner
    after = lax.rem(me + 1, group)
    before = lax.rem(me + group - 1, group)
    peers_1 = [row * inner + lax.rem(col + d, inner) for d in range(1, inner)]
    peers_2 = [lax.rem(row + d, outer) * inner + col for d in range(1, outer)]
    wins = (win_0, win_1, win_2, win_3)

    barrier = pltpu.get_barrier_semaphore()
    everyone = [after, before] + peers_1 + peers_2
    for peer in everyone:
        pl.semaphore_signal(barrier, inc=1, device_id={"gx": peer}, device_id_type=MESH)

    def ring_copy(src, dst, index, peer):
        return pltpu.make_async_remote_copy(
            src_ref=src,
            dst_ref=dst,
            send_sem=ring_send.at[index],
            recv_sem=ring_recv.at[index],
            device_id={"gx": peer},
            device_id_type=MESH,
        )

    def sum_copies(which, stage):
        buf = sums_1 if stage == 0 else sums_2
        at = col if stage == 0 else row
        peers = peers_1 if stage == 0 else peers_2
        base = which * (inner + outer) + stage * inner
        return [
            pltpu.make_async_remote_copy(
                src_ref=buf.at[which, at],
                dst_ref=buf.at[which, at],
                send_sem=sum_send.at[base + d],
                recv_sem=sum_recv.at[base + d],
                device_id={"gx": peer},
                device_id_type=MESH,
            )
            for d, peer in enumerate(peers)
        ]

    def sum_start(which, stage, value):
        buf = sums_1 if stage == 0 else sums_2
        buf[which, pl.ds(col if stage == 0 else row, 1)] = value[None]
        for copy in sum_copies(which, stage):
            copy.start()

    def sum_finish(which, stage):
        for copy in sum_copies(which, stage):
            copy.wait()
        buf = sums_1 if stage == 0 else sums_2
        total = buf[which, 0]
        for d in range(1, inner if stage == 0 else outer):
            total = total + buf[which, d]
        return total

    def inner_rows(a, b):
        return jnp.sum(a * b, axis=0, keepdims=True)

    sub_ids = lax.broadcasted_iota(jnp.int32, (16, 128), 0)
    lane_ids = lax.broadcasted_iota(jnp.int32, (16, 128), 1)

    def packed_sums(stack):
        totals = jnp.sum(stack, axis=1, keepdims=True)
        return jnp.sum(jnp.where(sub_ids == lane_ids, totals, 0.0), axis=0, keepdims=True)

    def unpacked(sums):
        gram[...] = jnp.broadcast_to(sums, (128, 128)).T

    rhs = rhs_ref[...]
    inv_alpha = inv_alpha_ref[...]
    inv_alpha_3 = jnp.concatenate([inv_alpha] * 3, axis=0)
    win_p[0 : 4 * tiles, :] = pack_ref[...]
    win_0[0 : 3 * tiles, :] = rhs
    colmat[...] = jnp.zeros((128, 128), F32)
    gram[...] = jnp.zeros((128, 128), F32)
    gram[0:1, :] = inner_rows(rhs, rhs)
    gram[1:2, :] = inner_rows(rhs, rhs * inv_alpha_3)

    def spread(buf, ref, index, count):
        for c in range(count):
            line = ref[pl.ds(c * tiles + index, 1), :]
            buf[c] = jnp.broadcast_to(line, (128, 128)).T

    def right_lines(n, vector):
        first = n + jnp.where(n >= tiles, 3 * tiles, 0)
        lines = [win_p[pl.ds(first + c * tiles, 1), :] for c in range(4)]
        if vector is not None:
            lines = [lines[c] + vector[c] for c in range(3)] + lines[3:]
        lines[3] = lines[3] * (-THOLE)
        return [jnp.broadcast_to(line, (ROWS, 128)) for line in lines]

    block_sub = lax.broadcasted_iota(jnp.int32, (ROWS, 128), 0)
    block_lane = lax.broadcasted_iota(jnp.int32, (ROWS, 128), 1)
    steps = 128 // ROWS

    def rows_of(i):
        return pl.ds(pl.multiple_of(i * ROWS, ROWS), ROWS)

    def own_tensors(t, cols):
        right = right_lines(t, None)

        def block(i, carry):
            left = [cols[c, rows_of(i), :] for c in range(4)]
            same = block_sub + i * ROWS == block_lane
            for k, value in enumerate(pair_tensor(left, right, same)):
                own_t[t, k, rows_of(i), :] = value
            return carry

        lax.fori_loop(0, steps, block, 0, unroll=True)

    last = me == group - 1

    def pair_tensors(t, cols):
        for e in range(2):
            n = list_ref[t, e + 1]
            wrap = jnp.where(jnp.logical_and(n >= tiles, last), 4.0 * group, 0.0)
            vector = (
                wrap,
                shift_ref[0, t, e + 1].astype(F32) * 128.0,
                shift_ref[1, t, e + 1].astype(F32) * (2.0 * tiles),
            )
            right = right_lines(n, vector)

            def block(i, carry):
                left = [cols[c, rows_of(i), :] for c in range(4)]
                for k, value in enumerate(pair_tensor(left, right, None)):
                    pair_t[t, e, k, rows_of(i), :] = value
                return carry

            lax.fori_loop(0, steps, block, 0, unroll=True)

    def in_pairs(ref, count, work):
        spread(cols_a, ref, 0, count)

        def body(u, carry):
            t = 2 * u
            spread(cols_b, ref, t + 1, count)
            work(t, cols_a)
            spread(cols_a, ref, lax.rem(t + 2, tiles), count)
            work(t + 1, cols_b)
            return carry

        lax.fori_loop(0, tiles // 2, body, 0)

    def own_fields(win):
        def body(t, carry):
            m = [
                jnp.broadcast_to(win[pl.ds(c * tiles + t, 1), :], (ROWS, 128))
                for c in range(3)
            ]

            def block(i, inside):
                tensor = [own_t[t, k, rows_of(i), :] for k in range(6)]
                for c, value in enumerate(times(tensor, m)):
                    part[t, c, rows_of(i), :] = value
                return inside

            lax.fori_loop(0, steps, block, 0, unroll=True)
            return carry

        lax.fori_loop(0, tiles, body, 0)

    def right_fields(win):
        def work(t, cols):
            def block(i, sums):
                m = [cols[c, rows_of(i), :] for c in range(3)]
                new = []
                for e in range(2):
                    tensor = [pair_t[t, e, k, rows_of(i), :] for k in range(6)]
                    new += list(times(tensor, m))
                return tuple(a + b for a, b in zip(sums, new))

            sums = lax.fori_loop(0, steps, block, (jnp.zeros((ROWS, 128), F32),) * 6, unroll=True)
            for e in range(2):
                for c in range(3):
                    right_rows[pl.ds(2 * tiles * c + 2 * t + e, 1), :] = jnp.sum(
                        sums[3 * e + c], axis=0, keepdims=True
                    )

        in_pairs(win, 3, work)
        rows = right_rows[...]
        rows = jnp.concatenate(
            [rows[2 * tiles * c : 2 * tiles * (c + 1)] for c in range(3)], axis=1
        )
        first = rows.astype(jnp.bfloat16)
        rows = rows - first.astype(F32)
        second = rows.astype(jnp.bfloat16)
        third = (rows - second.astype(F32)).astype(jnp.bfloat16)
        split = jnp.concatenate([first, second, third], axis=0)
        total = jnp.dot(hot[...], split, preferred_element_type=F32)
        return [
            jnp.concatenate([half[:, lanes(c)] for c in range(3)], axis=0)
            for half in (total[0:tiles], total[tiles : 2 * tiles])
        ]

    full_lane = lax.broadcasted_iota(jnp.int32, (128, 128), 1)

    def gather_column(t):
        now = colmat[...]
        for c in range(3):
            total = jnp.sum(part[t, c], axis=1, keepdims=True)
            now = jnp.where(full_lane == c * tiles + t, total, now)
        colmat[...] = now

    def left_fields(win):
        def body(t, carry):
            gather_column(lax.rem(t + tiles - 1, tiles))
            m = []
            for e in range(2):
                n = list_ref[t, e + 1]
                first = n + jnp.where(n >= tiles, 2 * tiles, 0)
                m.append(
                    [
                        jnp.broadcast_to(win[pl.ds(first + c * tiles, 1), :], (ROWS, 128))
                        for c in range(3)
                    ]
                )

            def block(i, inside):
                sums = [part[t, c, rows_of(i), :] for c in range(3)]
                for e in range(2):
                    tensor = [pair_t[t, e, k, rows_of(i), :] for k in range(6)]
                    sums = [a + b for a, b in zip(sums, times(tensor, m[e]))]
                for c in range(3):
                    part[t, c, rows_of(i), :] = sums[c]
                return inside

            lax.fori_loop(0, steps, block, 0, unroll=True)
            return carry

        lax.fori_loop(0, tiles, body, 0)
        gather_column(tiles - 1)
        return colmat[...].T[0 : 3 * tiles]

    in_pairs(pack_ref, 4, own_tensors)

    pl.semaphore_wait(barrier, len(everyone))
    halo_p = ring_copy(pack_ref, win_p.at[4 * tiles : 8 * tiles], 0, before)
    halo_p.start()
    halos = [ring_copy(rhs_ref, win_0.at[3 * tiles : 6 * tiles], 1, before)]
    halos += [
        ring_copy(wins[k].at[0 : 3 * tiles], wins[k].at[3 * tiles : 6 * tiles], 1 + k, before)
        for k in range(1, ITERS)
    ]
    returns = [
        ring_copy(ret_out.at[k], ret_in.at[k], 1 + ITERS + k, after) for k in range(ITERS)
    ]
    halos[0].start()
    sum_start(0, 0, packed_sums(gram[0:16, :]))

    own_fields(win_0)

    hot_lane = lax.broadcasted_iota(jnp.int32, (1, 128), 1)

    def mark(t, carry):
        for e in range(2):
            value = jnp.where(hot_lane == list_ref[t, e + 1], 1.0, 0.0)
            gram[pl.ds(2 * t + e, 1), :] = value
        return carry

    lax.fori_loop(0, tiles, mark, 0)
    marks = gram[...].T[0 : 2 * tiles, 0 : 2 * tiles].astype(jnp.bfloat16)
    hot[...] = jnp.concatenate([marks] * 3, axis=1)
    gram[...] = jnp.zeros((128, 128), F32)

    sum_start(0, 1, sum_finish(0, 0))
    halo_p.wait()
    in_pairs(pack_ref, 4, pair_tensors)

    vectors = [rhs]
    pair_index = {}
    centre = None
    centre_row = None
    for k in range(ITERS):
        if k > 0:
            halos[k].start()
        kept, sent = right_fields(wins[k])
        ret_out[k] = sent
        if k > 0:
            own_fields(wins[k])
        returns[k].start()
        halos[k].wait()
        field = left_fields(wins[k])
        field = field + kept
        if k == 0:
            unpacked(sum_finish(0, 1))
            centre_row = gram[1:2, :] / gram[0:1, :]
            gram[...] = jnp.zeros((128, 128), F32)
            gram[0:1, :] = inner_rows(rhs, rhs)
            pair_index[(0, 0)] = 0
            shifted = jnp.concatenate([inv_alpha - centre_row] * 3, axis=0)
        returns[k].wait()
        now = vectors[k]
        new = shifted * now - (field + ret_in[k])
        if k + 1 < ITERS:
            wins[k + 1][0 : 3 * tiles, :] = new
        else:
            top[...] = new
        vectors = []
        for j in range(k + 2):
            if j == ITERS:
                vectors.append(top[...])
            else:
                vectors.append(rhs_ref[...] if j == 0 else wins[j][0 : 3 * tiles, :])
        for j in range(k + 2):
            pair_index[(j, k + 1)] = len(pair_index)
            index = pair_index[(j, k + 1)]
            gram[index : index + 1, :] = inner_rows(vectors[j], new)

    sum_start(1, 0, packed_sums(gram[0:16, :]))
    sum_start(1, 1, sum_finish(1, 0))
    unpacked(sum_finish(1, 1))

    def entry(a, b):
        index = pair_index[(min(a, b), max(a, b))]
        return gram[index : index + 1, :]

    def form(a, b):
        out = None
        for i, p in enumerate(a):
            for j, q in enumerate(b):
                term = p * q * entry(i, j)
                out = term if out is None else out + term
        return out

    def plus(a, scale, b):
        out = []
        for i in range(max(len(a), len(b))):
            term = scale * b[i] if i < len(b) else None
            if i < len(a):
                out.append(a[i] if term is None else a[i] + term)
            else:
                out.append(term)
        return out

    one = jnp.ones((1, 128), F32)
    x_coef = []
    r_coef = [one]
    d_coef = [one]
    norm_now = form(r_coef, r_coef)
    for iteration in range(ITERS):
        applied = [centre_row * v for v in d_coef] + [0.0 * one]
        applied = [
            applied[i] + d_coef[i - 1] if i > 0 else applied[i] for i in range(len(applied))
        ]
        step = norm_now / form(d_coef, applied)
        x_coef = plus(x_coef, step, d_coef)
        r_coef = plus(r_coef, -step, applied)
        if iteration + 1 < ITERS:
            norm_next = form(r_coef, r_coef)
            d_coef = plus(r_coef, norm_next / norm_now, d_coef)
            norm_now = norm_next

    for out_ref, coef in ((x_ref, x_coef), (r_ref, r_coef)):
        total = None
        for j, value in enumerate(coef):
            term = value * vectors[j]
            total = term if total is None else total + term
        out_ref[...] = total


def on_device(group, positions, polar, field_ext, tile_atom, tile_list, image_shift):
    atoms = tile_atom.shape[0]
    tiles = tile_list.shape[0]
    inner = 16 if group % 16 == 0 else 2
    outer = group // inner
    vmem = pl.BlockSpec(memory_space=pltpu.VMEM)
    smem = pl.BlockSpec(memory_space=pltpu.SMEM)
    state = jax.ShapeDtypeStruct((3 * tiles, 128), F32)

    def shape(*dims, dtype=F32):
        return jax.ShapeDtypeStruct(dims, dtype)

    pack, inv_alpha, rhs, slot = pl.pallas_call(
        tiled_order_kernel,
        out_shape=(shape(4 * tiles, 128), shape(tiles, 128), state, shape(tiles, 128, dtype=jnp.int32)),
        in_specs=[vmem] * 4,
        out_specs=(vmem,) * 4,
        name="tiled_order",
    )(positions, polar.reshape(tiles, 128), field_ext, tile_atom.reshape(tiles, 128))

    sum_count = 2 * (inner + outer)
    ring_count = 1 + 2 * ITERS
    x, r = pl.pallas_call(
        functools.partial(solve_kernel, group, inner),
        out_shape=(state, state),
        in_specs=[vmem] * 3 + [smem] * 2,
        out_specs=(vmem,) * 2,
        scratch_shapes=[
            pltpu.VMEM((tiles, 6, 128, 128), F32),
            pltpu.VMEM((tiles, 2, 6, 128, 128), F32),
            pltpu.VMEM((tiles, 3, 128, 128), F32),
            pltpu.VMEM((4, 128, 128), F32),
            pltpu.VMEM((4, 128, 128), F32),
            pltpu.VMEM((8 * tiles, 128), F32),
        ]
        + [pltpu.VMEM((6 * tiles, 128), F32)] * ITERS
        + [
            pltpu.VMEM((3 * tiles, 128), F32),
            pltpu.VMEM((ITERS, 3 * tiles, 128), F32),
            pltpu.VMEM((ITERS, 3 * tiles, 128), F32),
            pltpu.VMEM((6 * tiles, 128), F32),
            pltpu.VMEM((2 * tiles, 6 * tiles), jnp.bfloat16),
            pltpu.VMEM((128, 128), F32),
            pltpu.VMEM((128, 128), F32),
            pltpu.VMEM((2, inner, 1, 128), F32),
            pltpu.VMEM((2, outer, 1, 128), F32),
            pltpu.SemaphoreType.DMA((ring_count,)),
            pltpu.SemaphoreType.DMA((ring_count,)),
            pltpu.SemaphoreType.DMA((sum_count,)),
            pltpu.SemaphoreType.DMA((sum_count,)),
        ],
        compiler_params=pltpu.CompilerParams(
            collective_id=0, has_side_effects=True, vmem_limit_bytes=60 * 1024 * 1024
        ),
        name="solve",
    )(pack, rhs, inv_alpha, tile_list, image_shift)

    return pl.pallas_call(
        atom_order_kernel,
        out_shape=(shape(3, atoms), shape(3, atoms)),
        in_specs=[vmem] * 3,
        out_specs=(vmem,) * 2,
        name="atom_order",
    )(x, r, slot)


def solution(mesh):
    both = ("rep", "gx")
    return jax.shard_map(
        functools.partial(on_device, mesh.shape["gx"]),
        mesh=mesh,
        in_specs=(
            P(None, both),
            P(both),
            P(None, both),
            P(both),
            P(both, None),
            P(None, both, None),
        ),
        out_specs=(P(None, both), P(None, both)),
        check_vma=False,
    )
```

time: 493 us -> 112 us (0.23)
  blocking collectives: 153 us -> 0 us
  local copies, waits for them, and re-layouts: 143 us -> 2.07 us
  Pallas kernels: 0 us -> 109 us
  other arithmetic: 104 us -> 0 us
  loops' own time: 25.6 us -> 0 us
  starting transfers between devices: 22.5 us -> 0 us
  waiting for transfers between devices: 21.1 us -> 0 us
  between operations: 15.3 us -> 0.65 us
  matrix products: 7.52 us -> 0 us
    psum x12 -> x0, blocking collectives: 153 us -> none  [over_axes(): return functools.reduce(lax.psum, axes, shard)]
    pallas_call x0 -> x3, Pallas kernels: none -> 109 us  [the longest x1 91.7 us: on_device(): pl.pallas_call(functools.partial(solve_kernel, group, inner), out_shape=(...]
    reduce_sum x16 -> x0, other arithmetic: 96.2 us -> none  [the longest x12 93.5 us: pair_block(): jnp.sum(lift_left * offsets[component] - coeff_three * moment_left[:, com...]
    gather x75 -> x0, local copies, waits for them, and re-layouts: 94.2 us -> none  [the longest x1 23 us: on_device(): tiled_polar = polar[tile_atom].reshape(tile_count, tile_width)]
    another operation x4 -> x0, loops' own time: 25.6 us -> none  [slab_fields(): lax.scan(accumulate, jnp.zeros((window_size, 3 * tile_width), jnp.float32...]
    scatter x2 -> x0, local copies, waits for them, and re-layouts: 23.1 us -> none  [the longest x1 11.6 us: on_device(): residual = jnp.zeros((3, atom_count), jnp.float32).at[:, tile_atom].set(r...]
    ppermute x9 -> x0, starting transfers between devices: 22.5 us -> none  [passed_along(): return lax.ppermute(value, axis, pairs)]
    ppermute x9 -> x0, waiting for transfers between devices: 21.1 us -> none  [passed_along(): return lax.ppermute(value, axis, pairs)]
  transfers between devices with their start and end apart: 9 -> 0, of which waited for: 8 -> 0; matrix products, arithmetic and copies ran while one was open for 4% -> 0% of each run, Pallas kernels for 0% -> 0%
where the time goes in v1:
time: 112 us; the launch traced here: 111 us
  Pallas kernels  109 us (97%)
  local copies, waits for them, and re-layouts  2.07 us (2%)
    pallas_call x1, Pallas kernels, on_device(): pl.pallas_call(functools.partial(solve_kernel, group, inner), out_shape=(...  91.7 us
    pallas_call x1, Pallas kernels, on_device(): pl.pallas_call(tiled_order_kernel, out_shape=(shape(4 * tiles, 128), shap...  11.3 us
    pallas_call x1, Pallas kernels, on_device(): pl.pallas_call(atom_order_kernel, out_shape=(shape(3, atoms), shape(3, at...  5.72 us

profile of v1, /device:TPU:513, one launch (start us, length us, event | category | flops | bytes accessed | tf_op | source)
XLA Modules:
  0.0 111.5 jit_solution(15096460154196394068)
XLA Ops:
  0.6 0.0 copy-start.1
  0.6 0.7 copy-done.1
  1.3 0.0 copy-start
  1.3 0.7 copy.8.list_ref
  2.0 0.0 copy-done
  2.0 0.7 copy.9.shift_ref
  2.7 11.3 %tiled_order.1 = (f32[128,128]{1,0:T(8,128)}, f32[32,128]{1,0:T(8,128)}, f32[96,128]{1,0:T(8,128)}, s32[32,128]{1,0:T(8,128)}) custom-call(f32[3,4096]{1,0:T(4,128)} %pos_ref.1, f32[32,128]{1,0:T(8,128)} %bitcast.2, f32[3,4096]{1,0:T(4,128)} %field_ref.1, s32[32,128]{1,0:T(8,128)} %bitcast.3), custom_call_target="tpu_custom_call" | custom-call | tf_op jit(solution)/shard_map/tiled_order/pallas_call | solution.py:539
  14.0 91.7 %solve.1 = (f32[96,128]{1,0:T(8,128)}, f32[96,128]{1,0:T(8,128)}) custom-call(f32[128,128]{1,0:T(8,128)} %get-tuple-element.8.pack_ref, f32[96,128]{1,0:T(8,128)} %get-tuple-element.9.rhs_ref, f32[32,128]{1,0:T(8,128)} %get-tuple-element.10.inv_alpha_ref, s32[32,3]{1,0:T(8,128)} %copy.8.list_ref, s32[2,32,3]{2,1,0:T(8,128)} %copy.9.shift_ref), custom_call_target="tpu_custom_call" | custom-call | tf_op jit(solution)/shard_map/solve/pallas_call | solution.py:549
  105.7 5.7 %atom_order.1 = (f32[3,4096]{1,0:T(4,128)}, f32[3,4096]{1,0:T(4,128)}) custom-call(f32[96,128]{1,0:T(8,128)} %get-tuple-element.11.x_ref, f32[96,128]{1,0:T(8,128)} %get-tuple-element.12.r_ref, s32[32,128]{1,0:T(8,128)} %get-tuple-element.13.slot_ref), custom_call_target="tpu_custom_call" | custom-call | tf_op jit(solution)/shard_map/atom_order/pallas_call | solution.py:584
Async XLA Ops:
  0.6 0.7 copy-start.1
  1.3 0.7 copy-start

commit v2 on v1

--- a/solution.py
+++ b/solution.py
@@ -18,76 +18,83 @@
     return slice(index * 128, (index + 1) * 128)
 
 
+def gathered(slot, rows_at, count, steps):
+    blocks = []
+    for start in range(0, slot.shape[0], 8):
+        index = slot[start : start + 8]
+        high = lax.shift_right_logical(index, 7)
+        low = jnp.bitwise_and(index, 127)
+
+        def pick(step, found):
+            hit = high == step
+            return tuple(
+                jnp.where(
+                    hit,
+                    jnp.take_along_axis(jnp.broadcast_to(row, (8, 128)), low, axis=1),
+                    old,
+                )
+                for row, old in zip(rows_at(step), found)
+            )
+
+        zero = jnp.zeros((8, 128), F32)
+        blocks.append(lax.fori_loop(0, steps, pick, (zero,) * count, unroll=True))
+    return blocks
+
+
 def tiled_order_kernel(pos_ref, polar_ref, field_ref, atom_ref, pack_ref, inv_alpha_ref, rhs_ref, slot_ref):
     tiles = atom_ref.shape[0]
     atom = atom_ref[...]
-    high = atom // 128
-    low = atom % 128
-
-    def pick(step, found):
-        hit = high == step
+
+    def rows_at(step):
         cols = pl.ds(pl.multiple_of(step * 128, 128), 128)
         rows = [pos_ref[c : c + 1, cols] for c in range(3)]
         rows += [field_ref[c : c + 1, cols] for c in range(3)]
-        rows.append(polar_ref[pl.ds(step, 1), :])
-        new = []
-        for row, old in zip(rows, found):
-            wide = jnp.broadcast_to(row, (tiles, 128))
-            new.append(jnp.where(hit, jnp.take_along_axis(wide, low, axis=1), old))
-        return tuple(new)
-
-    zero = jnp.zeros((tiles, 128), F32)
-    found = lax.fori_loop(0, tiles, pick, (zero,) * 7)
-    for c in range(3):
-        pack_ref[c * tiles : (c + 1) * tiles, :] = found[c]
-        rhs_ref[c * tiles : (c + 1) * tiles, :] = found[3 + c]
-    pack_ref[3 * tiles : 4 * tiles, :] = lax.rsqrt(found[6])
-    inv_alpha_ref[...] = 1.0 / found[6]
+        return rows + [polar_ref[pl.ds(step, 1), :]]
+
+    for block, found in enumerate(gathered(atom, rows_at, 7, tiles)):
+        for c in range(3):
+            pack_ref[c * tiles + 8 * block : c * tiles + 8 * block + 8, :] = found[c]
+            rhs_ref[c * tiles + 8 * block : c * tiles + 8 * block + 8, :] = found[3 + c]
+        pack_ref[3 * tiles + 8 * block : 3 * tiles + 8 * block + 8, :] = lax.rsqrt(found[6])
+        inv_alpha_ref[8 * block : 8 * block + 8, :] = 1.0 / found[6]
 
     high_ids = lax.broadcasted_iota(jnp.int32, (tiles, 128), 0)
     low_ids = lax.broadcasted_iota(jnp.int32, (128, 128), 0)
     lane_ids = lax.broadcasted_iota(jnp.int32, (tiles, 128), 1).astype(F32)
-
-    def invert(step, total):
-        row = atom_ref[pl.ds(step, 1), :]
-        hot_high = high_ids == row // 128
-        hot_low = jnp.where(low_ids == row % 128, 1.0, 0.0).astype(jnp.bfloat16)
-        left = jnp.concatenate(
-            [
-                jnp.where(hot_high, lax.convert_element_type(step, F32), 0.0),
-                jnp.where(hot_high, lane_ids, 0.0),
-            ],
-            axis=0,
-        ).astype(jnp.bfloat16)
-        return total + lax.dot_general(
-            left, hot_low, (((1,), (1,)), ((), ())), preferred_element_type=F32
+    high = lax.shift_right_logical(atom, 7)
+    low = jnp.bitwise_and(atom, 127)
+    total = None
+    for pair in range(0, tiles, 2):
+        left, right = [], []
+        for step in (pair, pair + 1):
+            hot = high_ids == high[step : step + 1]
+            left.append(
+                jnp.concatenate(
+                    [jnp.where(hot, float(step), 0.0), jnp.where(hot, lane_ids, 0.0)], axis=0
+                )
+            )
+            right.append(jnp.where(low_ids == low[step : step + 1], 1.0, 0.0))
+        term = lax.dot_general(
+            jnp.concatenate(left, axis=1).astype(jnp.bfloat16),
+            jnp.concatenate(right, axis=1).astype(jnp.bfloat16),
+            (((1,), (1,)), ((), ())),
+            preferred_element_type=F32,
         )
-
-    total = lax.fori_loop(0, tiles, invert, jnp.zeros((2 * tiles, 128), F32))
+        total = term if total is None else total + term
     slot_ref[...] = (total[:tiles] * 128.0 + total[tiles:]).astype(jnp.int32)
 
 
 def atom_order_kernel(x_ref, r_ref, slot_ref, dipoles_ref, residual_ref):
     tiles = slot_ref.shape[0]
-    slot = slot_ref[...]
-    high = slot // 128
-    low = slot % 128
-
-    def pick(step, found):
-        hit = high == step
-        rows = [ref[pl.ds(c * tiles + step, 1), :] for ref in (x_ref, r_ref) for c in range(3)]
-        new = []
-        for row, old in zip(rows, found):
-            wide = jnp.broadcast_to(row, (tiles, 128))
-            new.append(jnp.where(hit, jnp.take_along_axis(wide, low, axis=1), old))
-        return tuple(new)
-
-    zero = jnp.zeros((tiles, 128), F32)
-    found = lax.fori_loop(0, tiles, pick, (zero,) * 6)
-    for c in range(3):
-        for h in range(tiles):
-            dipoles_ref[c : c + 1, lanes(h)] = found[c][h : h + 1, :]
-            residual_ref[c : c + 1, lanes(h)] = found[3 + c][h : h + 1, :]
+
+    def rows_at(step):
+        return [ref[pl.ds(c * tiles + step, 1), :] for ref in (x_ref, r_ref) for c in range(3)]
+
+    for block, found in enumerate(gathered(slot_ref[...], rows_at, 6, tiles)):
+        for c in range(3):
+            for h in range(8):
+                dipoles_ref[c : c + 1, lanes(8 * block + h)] = found[c][h : h + 1, :]
+                residual_ref[c : c + 1, lanes(8 * block + h)] = found[3 + c][h : h + 1, :]
 
 
 def pair_tensor(left, right, diagonal):
@@ -241,10 +248,12 @@
     gram[0:1, :] = inner_rows(rhs, rhs)
     gram[1:2, :] = inner_rows(rhs, rhs * inv_alpha_3)
 
+    steps = 128 // ROWS
+
     def spread(buf, ref, index, count):
         for c in range(count):
             line = ref[pl.ds(c * tiles + index, 1), :]
-            buf[c] = jnp.broadcast_to(line, (128, 128)).T
+            buf[:, c] = jnp.broadcast_to(line, (128, 128)).T.reshape(steps, ROWS, 128)
 
     def right_lines(n, vector):
         first = n + jnp.where(n >= tiles, 3 * tiles, 0)
@@ -256,19 +265,15 @@
 
     block_sub = lax.broadcasted_iota(jnp.int32, (ROWS, 128), 0)
     block_lane = lax.broadcasted_iota(jnp.int32, (ROWS, 128), 1)
-    steps = 128 // ROWS
-
-    def rows_of(i):
-        return pl.ds(pl.multiple_of(i * ROWS, ROWS), ROWS)
 
     def own_tensors(t, cols):
         right = right_lines(t, None)
 
         def block(i, carry):
-            left = [cols[c, rows_of(i), :] for c in range(4)]
+            left = [cols[i, c] for c in range(4)]
             same = block_sub + i * ROWS == block_lane
             for k, value in enumerate(pair_tensor(left, right, same)):
-                own_t[t, k, rows_of(i), :] = value
+                own_t[t, i, k] = value
             return carry
 
         lax.fori_loop(0, steps, block, 0, unroll=True)
@@ -287,9 +292,9 @@
             right = right_lines(n, vector)
 
             def block(i, carry):
-                left = [cols[c, rows_of(i), :] for c in range(4)]
+                left = [cols[i, c] for c in range(4)]
                 for k, value in enumerate(pair_tensor(left, right, None)):
-                    pair_t[t, e, k, rows_of(i), :] = value
+                    pair_t[t, e, i, k] = value
                 return carry
 
             lax.fori_loop(0, steps, block, 0, unroll=True)
@@ -315,9 +320,9 @@
             ]
 
             def block(i, inside):
-                tensor = [own_t[t, k, rows_of(i), :] for k in range(6)]
+                tensor = [own_t[t, i, k] for k in range(6)]
                 for c, value in enumerate(times(tensor, m)):
-                    part[t, c, rows_of(i), :] = value
+                    part[t, i, c] = value
                 return inside
 
             lax.fori_loop(0, steps, block, 0, unroll=True)
@@ -328,10 +333,10 @@
     def right_fields(win):
         def work(t, cols):
             def block(i, sums):
-                m = [cols[c, rows_of(i), :] for c in range(3)]
+                m = [cols[i, c] for c in range(3)]
                 new = []
                 for e in range(2):
-                    tensor = [pair_t[t, e, k, rows_of(i), :] for k in range(6)]
+                    tensor = [pair_t[t, e, i, k] for k in range(6)]
                     new += list(times(tensor, m))
                 return tuple(a + b for a, b in zip(sums, new))
 
@@ -363,12 +368,12 @@
     def gather_column(t):
         now = colmat[...]
         for c in range(3):
-            total = jnp.sum(part[t, c], axis=1, keepdims=True)
+            total = jnp.sum(part[t, :, c].reshape(128, 128), axis=1, keepdims=True)
             now = jnp.where(full_lane == c * tiles + t, total, now)
         colmat[...] = now
 
     def left_fields(win):
-        def body(t, carry):
+        def one(t):
             gather_column(lax.rem(t + tiles - 1, tiles))
             m = []
             for e in range(2):
@@ -382,18 +387,22 @@
                 )
 
             def block(i, inside):
-                sums = [part[t, c, rows_of(i), :] for c in range(3)]
+                sums = [part[t, i, c] for c in range(3)]
                 for e in range(2):
-                    tensor = [pair_t[t, e, k, rows_of(i), :] for k in range(6)]
+                    tensor = [pair_t[t, e, i, k] for k in range(6)]
                     sums = [a + b for a, b in zip(sums, times(tensor, m[e]))]
                 for c in range(3):
-                    part[t, c, rows_of(i), :] = sums[c]
+                    part[t, i, c] = sums[c]
                 return inside
 
             lax.fori_loop(0, steps, block, 0, unroll=True)
+
+        def body(u, carry):
+            for step in range(4):
+                one(4 * u + step)
             return carry
 
-        lax.fori_loop(0, tiles, body, 0)
+        lax.fori_loop(0, tiles // 4, body, 0)
         gather_column(tiles - 1)
         return colmat[...].T[0 : 3 * tiles]
 
@@ -529,6 +538,7 @@
     tiles = tile_list.shape[0]
     inner = 16 if group % 16 == 0 else 2
     outer = group // inner
+    steps = 128 // ROWS
     vmem = pl.BlockSpec(memory_space=pltpu.VMEM)
     smem = pl.BlockSpec(memory_space=pltpu.SMEM)
     state = jax.ShapeDtypeStruct((3 * tiles, 128), F32)
@@ -552,11 +562,11 @@
         in_specs=[vmem] * 3 + [smem] * 2,
         out_specs=(vmem,) * 2,
         scratch_shapes=[
-            pltpu.VMEM((tiles, 6, 128, 128), F32),
-            pltpu.VMEM((tiles, 2, 6, 128, 128), F32),
-            pltpu.VMEM((tiles, 3, 128, 128), F32),
-            pltpu.VMEM((4, 128, 128), F32),
-            pltpu.VMEM((4, 128, 128), F32),
+            pltpu.VMEM((tiles, steps, 6, ROWS, 128), F32),
+            pltpu.VMEM((tiles, 2, steps, 6, ROWS, 128), F32),
+            pltpu.VMEM((tiles, steps, 3, ROWS, 128), F32),
+            pltpu.VMEM((steps, 4, ROWS, 128), F32),
+            pltpu.VMEM((steps, 4, ROWS, 128), F32),
             pltpu.VMEM((8 * tiles, 128), F32),
         ]
         + [pltpu.VMEM((6 * tiles, 128), F32)] * ITERS

time: 112 us -> 90.9 us (0.81)
  Pallas kernels: 109 us -> 87.8 us
    pallas_call x1, Pallas kernels: 91.7 us -> 82.8 us  [on_device(): pl.pallas_call(functools.partial(solve_kernel, group, inner), out_shape=(...]
    pallas_call x1, Pallas kernels: 11.3 us -> 2.63 us  [on_device(): pl.pallas_call(tiled_order_kernel, out_shape=(shape(4 * tiles, 128), shap...]
    pallas_call x1, Pallas kernels: 5.72 us -> 2.38 us  [on_device(): pl.pallas_call(atom_order_kernel, out_shape=(shape(3, atoms), shape(3, at...]
where the time goes in v2:
time: 90.9 us; the launch traced here: 90.5 us
  Pallas kernels  87.8 us (97%)
  local copies, waits for them, and re-layouts  2.07 us (2%)
    pallas_call x1, Pallas kernels, on_device(): pl.pallas_call(functools.partial(solve_kernel, group, inner), out_shape=(...  82.8 us
    pallas_call x1, Pallas kernels, on_device(): pl.pallas_call(tiled_order_kernel, out_shape=(shape(4 * tiles, 128), shap...  2.63 us
    pallas_call x1, Pallas kernels, on_device(): pl.pallas_call(atom_order_kernel, out_shape=(shape(3, atoms), shape(3, at...  2.38 us
    unnamed x6, local copies, waits for them, and re-layouts  2.07 us

profile of v2, /device:TPU:513, one launch (start us, length us, event | category | flops | bytes accessed | tf_op | source)
XLA Modules:
  0.0 90.5 jit_solution(11668119032332245959)
XLA Ops:
  0.6 0.0 copy-start.1
  0.6 0.7 copy-done.1
  1.3 0.0 copy-start
  1.3 0.7 copy.8.list_ref
  2.0 0.0 copy-done
  2.0 0.7 copy.9.shift_ref
  2.7 2.6 %tiled_order.1 = (f32[128,128]{1,0:T(8,128)}, f32[32,128]{1,0:T(8,128)}, f32[96,128]{1,0:T(8,128)}, s32[32,128]{1,0:T(8,128)}) custom-call(f32[3,4096]{1,0:T(4,128)} %pos_ref.1, f32[32,128]{1,0:T(8,128)} %bitcast.2, f32[3,4096]{1,0:T(4,128)} %field_ref.1, s32[32,128]{1,0:T(8,128)} %bitcast.3), custom_call_target="tpu_custom_call" | custom-call | tf_op jit(solution)/shard_map/tiled_order/pallas_call | solution.py:549
  5.3 82.8 %solve.1 = (f32[96,128]{1,0:T(8,128)}, f32[96,128]{1,0:T(8,128)}) custom-call(f32[128,128]{1,0:T(8,128)} %get-tuple-element.8.pack_ref, f32[96,128]{1,0:T(8,128)} %get-tuple-element.9.rhs_ref, f32[32,128]{1,0:T(8,128)} %get-tuple-element.10.inv_alpha_ref, s32[32,3]{1,0:T(8,128)} %copy.8.list_ref, s32[2,32,3]{2,1,0:T(8,128)} %copy.9.shift_ref), custom_call_target="tpu_custom_call" | custom-call | tf_op jit(solution)/shard_map/solve/pallas_call | solution.py:559
  88.2 2.4 %atom_order.1 = (f32[3,4096]{1,0:T(4,128)}, f32[3,4096]{1,0:T(4,128)}) custom-call(f32[96,128]{1,0:T(8,128)} %get-tuple-element.11.x_ref, f32[96,128]{1,0:T(8,128)} %get-tuple-element.12.r_ref, s32[32,128]{1,0:T(8,128)} %get-tuple-element.13.slot_ref), custom_call_target="tpu_custom_call" | custom-call | tf_op jit(solution)/shard_map/atom_order/pallas_call | solution.py:594
Async XLA Ops:
  0.6 0.7 copy-start.1
  1.3 0.7 copy-start

commit v3 on v2

--- a/solution.py
+++ b/solution.py
@@ -41,23 +41,8 @@
     return blocks
 
 
-def tiled_order_kernel(pos_ref, polar_ref, field_ref, atom_ref, pack_ref, inv_alpha_ref, rhs_ref, slot_ref):
-    tiles = atom_ref.shape[0]
-    atom = atom_ref[...]
-
-    def rows_at(step):
-        cols = pl.ds(pl.multiple_of(step * 128, 128), 128)
-        rows = [pos_ref[c : c + 1, cols] for c in range(3)]
-        rows += [field_ref[c : c + 1, cols] for c in range(3)]
-        return rows + [polar_ref[pl.ds(step, 1), :]]
-
-    for block, found in enumerate(gathered(atom, rows_at, 7, tiles)):
-        for c in range(3):
-            pack_ref[c * tiles + 8 * block : c * tiles + 8 * block + 8, :] = found[c]
-            rhs_ref[c * tiles + 8 * block : c * tiles + 8 * block + 8, :] = found[3 + c]
-        pack_ref[3 * tiles + 8 * block : 3 * tiles + 8 * block + 8, :] = lax.rsqrt(found[6])
-        inv_alpha_ref[8 * block : 8 * block + 8, :] = 1.0 / found[6]
-
+def inverse_order(atom):
+    tiles = atom.shape[0]
     high_ids = lax.broadcasted_iota(jnp.int32, (tiles, 128), 0)
     low_ids = lax.broadcasted_iota(jnp.int32, (128, 128), 0)
     lane_ids = lax.broadcasted_iota(jnp.int32, (tiles, 128), 1).astype(F32)
@@ -81,7 +66,7 @@
             preferred_element_type=F32,
         )
         total = term if total is None else total + term
-    slot_ref[...] = (total[:tiles] * 128.0 + total[tiles:]).astype(jnp.int32)
+    return (total[:tiles] * 128.0 + total[tiles:]).astype(jnp.int32)
 
 
 def atom_order_kernel(x_ref, r_ref, slot_ref, dipoles_ref, residual_ref):
@@ -137,13 +122,16 @@
 def solve_kernel(
     group,
     inner,
-    pack_ref,
-    rhs_ref,
-    inv_alpha_ref,
+    pos_ref,
+    polar_ref,
+    field_ref,
+    atom_ref,
     list_ref,
     shift_ref,
     x_ref,
     r_ref,
+    slot_ref,
+    inv_alpha_ref,
     own_t,
     pair_t,
     part,
@@ -158,6 +146,7 @@
     ret_out,
     ret_in,
     right_rows,
+    own_rows,
     hot,
     colmat,
     gram,
@@ -168,7 +157,7 @@
     sum_send,
     sum_recv,
 ):
-    tiles = rhs_ref.shape[0] // 3
+    tiles = atom_ref.shape[0]
     me = lax.axis_index("gx")
     outer = group // inner
     row, col = me // inner, me % inner
@@ -238,11 +227,24 @@
     def unpacked(sums):
         gram[...] = jnp.broadcast_to(sums, (128, 128)).T
 
-    rhs = rhs_ref[...]
+    def rows_at(step):
+        places = pl.ds(pl.multiple_of(step * 128, 128), 128)
+        rows = [pos_ref[c : c + 1, places] for c in range(3)]
+        rows += [field_ref[c : c + 1, places] for c in range(3)]
+        return rows + [polar_ref[pl.ds(step, 1), :]]
+
+    for block, found in enumerate(gathered(atom_ref[...], rows_at, 7, tiles)):
+        for c in range(3):
+            at = c * tiles + 8 * block
+            win_p[at : at + 8, :] = found[c]
+            win_0[at : at + 8, :] = found[3 + c]
+        at = 3 * tiles + 8 * block
+        win_p[at : at + 8, :] = lax.rsqrt(found[6])
+        inv_alpha_ref[8 * block : 8 * block + 8, :] = 1.0 / found[6]
+
+    rhs = win_0[0 : 3 * tiles, :]
     inv_alpha = inv_alpha_ref[...]
     inv_alpha_3 = jnp.concatenate([inv_alpha] * 3, axis=0)
-    win_p[0 : 4 * tiles, :] = pack_ref[...]
-    win_0[0 : 3 * tiles, :] = rhs
     colmat[...] = jnp.zeros((128, 128), F32)
     gram[...] = jnp.zeros((128, 128), F32)
     gram[0:1, :] = inner_rows(rhs, rhs)
@@ -282,12 +284,12 @@
 
     def pair_tensors(t, cols):
         for e in range(2):
-            n = list_ref[t, e + 1]
+            n = list_ref[e + 1, t]
             wrap = jnp.where(jnp.logical_and(n >= tiles, last), 4.0 * group, 0.0)
             vector = (
                 wrap,
-                shift_ref[0, t, e + 1].astype(F32) * 128.0,
-                shift_ref[1, t, e + 1].astype(F32) * (2.0 * tiles),
+                shift_ref[e + 1, 0, t].astype(F32) * 128.0,
+                shift_ref[e + 1, 1, t].astype(F32) * (2.0 * tiles),
             )
             right = right_lines(n, vector)
 
@@ -299,20 +301,20 @@
 
             lax.fori_loop(0, steps, block, 0, unroll=True)
 
-    def in_pairs(ref, count, work):
-        spread(cols_a, ref, 0, count)
+    def in_pairs(ref, count, work, first=0, stop=tiles):
+        spread(cols_a, ref, first, count)
 
         def body(u, carry):
-            t = 2 * u
+            t = first + 2 * u
             spread(cols_b, ref, t + 1, count)
             work(t, cols_a)
             spread(cols_a, ref, lax.rem(t + 2, tiles), count)
             work(t + 1, cols_b)
             return carry
 
-        lax.fori_loop(0, tiles // 2, body, 0)
-
-    def own_fields(win):
+        lax.fori_loop(0, (stop - first) // 2, body, 0)
+
+    def own_fields(win, first=0, stop=tiles):
         def body(t, carry):
             m = [
                 jnp.broadcast_to(win[pl.ds(c * tiles + t, 1), :], (ROWS, 128))
@@ -328,19 +330,27 @@
             lax.fori_loop(0, steps, block, 0, unroll=True)
             return carry
 
-        lax.fori_loop(0, tiles, body, 0)
-
-    def right_fields(win):
+        lax.fori_loop(first, stop, body, 0)
+
+    def right_fields(win, with_own):
+        sources = 3 if with_own else 2
+
         def work(t, cols):
             def block(i, sums):
                 m = [cols[i, c] for c in range(3)]
                 new = []
-                for e in range(2):
-                    tensor = [pair_t[t, e, i, k] for k in range(6)]
+                for e in range(sources):
+                    tensor = [own_t[t, i, k] if e == 2 else pair_t[t, e, i, k] for k in range(6)]
                     new += list(times(tensor, m))
                 return tuple(a + b for a, b in zip(sums, new))
 
-            sums = lax.fori_loop(0, steps, block, (jnp.zeros((ROWS, 128), F32),) * 6, unroll=True)
+            zeros = (jnp.zeros((ROWS, 128), F32),) * (3 * sources)
+            sums = lax.fori_loop(0, steps, block, zeros, unroll=True)
+            if with_own:
+                for c in range(3):
+                    own_rows[pl.ds(c * tiles + t, 1), :] = jnp.sum(
+                        sums[6 + c], axis=0, keepdims=True
+                    )
             for e in range(2):
                 for c in range(3):
                     right_rows[pl.ds(2 * tiles * c + 2 * t + e, 1), :] = jnp.sum(
@@ -372,12 +382,12 @@
             now = jnp.where(full_lane == c * tiles + t, total, now)
         colmat[...] = now
 
-    def left_fields(win):
+    def left_fields(win, with_part):
         def one(t):
             gather_column(lax.rem(t + tiles - 1, tiles))
             m = []
             for e in range(2):
-                n = list_ref[t, e + 1]
+                n = list_ref[e + 1, t]
                 first = n + jnp.where(n >= tiles, 2 * tiles, 0)
                 m.append(
                     [
@@ -387,10 +397,11 @@
                 )
 
             def block(i, inside):
-                sums = [part[t, i, c] for c in range(3)]
+                sums = [part[t, i, c] for c in range(3)] if with_part else None
                 for e in range(2):
                     tensor = [pair_t[t, e, i, k] for k in range(6)]
-                    sums = [a + b for a, b in zip(sums, times(tensor, m[e]))]
+                    new = times(tensor, m[e])
+                    sums = new if sums is None else [a + b for a, b in zip(sums, new)]
                 for c in range(3):
                     part[t, i, c] = sums[c]
                 return inside
@@ -406,15 +417,15 @@
         gather_column(tiles - 1)
         return colmat[...].T[0 : 3 * tiles]
 
-    in_pairs(pack_ref, 4, own_tensors)
+    in_pairs(win_p, 4, own_tensors, 0, tiles // 2)
 
     pl.semaphore_wait(barrier, len(everyone))
-    halo_p = ring_copy(pack_ref, win_p.at[4 * tiles : 8 * tiles], 0, before)
+    own_p, own_v = 4 * tiles, 3 * tiles
+    halo_p = ring_copy(win_p.at[0:own_p], win_p.at[own_p : 2 * own_p], 0, before)
     halo_p.start()
-    halos = [ring_copy(rhs_ref, win_0.at[3 * tiles : 6 * tiles], 1, before)]
-    halos += [
-        ring_copy(wins[k].at[0 : 3 * tiles], wins[k].at[3 * tiles : 6 * tiles], 1 + k, before)
-        for k in range(1, ITERS)
+    halos = [
+        ring_copy(win.at[0:own_v], win.at[own_v : 2 * own_v], 1 + k, before)
+        for k, win in enumerate(wins)
     ]
     returns = [
         ring_copy(ret_out.at[k], ret_in.at[k], 1 + ITERS + k, after) for k in range(ITERS)
@@ -422,13 +433,14 @@
     halos[0].start()
     sum_start(0, 0, packed_sums(gram[0:16, :]))
 
+    in_pairs(win_p, 4, own_tensors, tiles // 2, tiles)
     own_fields(win_0)
 
     hot_lane = lax.broadcasted_iota(jnp.int32, (1, 128), 1)
 
     def mark(t, carry):
         for e in range(2):
-            value = jnp.where(hot_lane == list_ref[t, e + 1], 1.0, 0.0)
+            value = jnp.where(hot_lane == list_ref[e + 1, t], 1.0, 0.0)
             gram[pl.ds(2 * t + e, 1), :] = value
         return carry
 
@@ -436,54 +448,64 @@
     marks = gram[...].T[0 : 2 * tiles, 0 : 2 * tiles].astype(jnp.bfloat16)
     hot[...] = jnp.concatenate([marks] * 3, axis=1)
     gram[...] = jnp.zeros((128, 128), F32)
-
+    slot_ref[...] = inverse_order(atom_ref[...])
+
+    halo_p.wait()
+    in_pairs(win_p, 4, pair_tensors)
     sum_start(0, 1, sum_finish(0, 0))
-    halo_p.wait()
-    in_pairs(pack_ref, 4, pair_tensors)
-
-    vectors = [rhs]
+
+    def own_vector(k):
+        return wins[k][0:own_v, :]
+
     pair_index = {}
+
+    def keep(key, line):
+        index = pair_index[key] = len(pair_index)
+        gram[index : index + 1, :] = line
+
     centre = None
-    centre_row = None
     for k in range(ITERS):
+        final = k + 1 == ITERS
         if k > 0:
+            for j in range(k + 1):
+                keep((j, k), inner_rows(own_vector(j), own_vector(k)))
             halos[k].start()
-        kept, sent = right_fields(wins[k])
+        kept, sent = right_fields(wins[k], final)
         ret_out[k] = sent
-        if k > 0:
-            own_fields(wins[k])
+        if k > 0 and not final:
+            own_fields(wins[k], 0, 4)
+        if final:
+            now = own_vector(k)
+            line = inner_rows(now, shifted * now - (own_rows[...] + 2.0 * kept))
+            kept = kept + own_rows[...]
         returns[k].start()
+        if k > 0 and not final:
+            own_fields(wins[k], 4, tiles)
         halos[k].wait()
-        field = left_fields(wins[k])
-        field = field + kept
+        if final:
+            line = line - 2.0 * inner_rows(wins[k][own_v : 2 * own_v, :], sent)
+            keep((k, k + 1), line)
+            sum_start(1, 0, packed_sums(gram[0:16, :]))
+        field = left_fields(wins[k], not final) + kept
         if k == 0:
             unpacked(sum_finish(0, 1))
-            centre_row = gram[1:2, :] / gram[0:1, :]
+            centre = gram[1:2, :] / gram[0:1, :]
             gram[...] = jnp.zeros((128, 128), F32)
-            gram[0:1, :] = inner_rows(rhs, rhs)
-            pair_index[(0, 0)] = 0
-            shifted = jnp.concatenate([inv_alpha - centre_row] * 3, axis=0)
+            keep((0, 0), inner_rows(rhs, rhs))
+            shifted = jnp.concatenate([inv_alpha - centre] * 3, axis=0)
+        if final:
+            sum_start(1, 1, sum_finish(1, 0))
         returns[k].wait()
-        now = vectors[k]
-        new = shifted * now - (field + ret_in[k])
-        if k + 1 < ITERS:
-            wins[k + 1][0 : 3 * tiles, :] = new
+        new = shifted * own_vector(k) - (field + ret_in[k])
+        if final:
+            top[...] = new
         else:
-            top[...] = new
-        vectors = []
-        for j in range(k + 2):
-            if j == ITERS:
-                vectors.append(top[...])
-            else:
-                vectors.append(rhs_ref[...] if j == 0 else wins[j][0 : 3 * tiles, :])
-        for j in range(k + 2):
-            pair_index[(j, k + 1)] = len(pair_index)
-            index = pair_index[(j, k + 1)]
-            gram[index : index + 1, :] = inner_rows(vectors[j], new)
-
-    sum_start(1, 0, packed_sums(gram[0:16, :]))
-    sum_start(1, 1, sum_finish(1, 0))
+            wins[k + 1][0:own_v, :] = new
+
     unpacked(sum_finish(1, 1))
+    vectors = [own_vector(k) for k in range(ITERS)] + [top[...]]
+    for j in range(ITERS - 1):
+        pair_index[(j, ITERS)] = pair_index[(j + 1, ITERS - 1)]
 
     def entry(a, b):
         index = pair_index[(min(a, b), max(a, b))]
@@ -513,7 +535,7 @@
     d_coef = [one]
     norm_now = form(r_coef, r_coef)
     for iteration in range(ITERS):
-        applied = [centre_row * v for v in d_coef] + [0.0 * one]
+        applied = [centre * v for v in d_coef] + [0.0 * one]
         applied = [
             applied[i] + d_coef[i - 1] if i > 0 else applied[i] for i in range(len(applied))
         ]
@@ -546,22 +568,15 @@
     def shape(*dims, dtype=F32):
         return jax.ShapeDtypeStruct(dims, dtype)
 
-    pack, inv_alpha, rhs, slot = pl.pallas_call(
-        tiled_order_kernel,
-        out_shape=(shape(4 * tiles, 128), shape(tiles, 128), state, shape(tiles, 128, dtype=jnp.int32)),
-        in_specs=[vmem] * 4,
-        out_specs=(vmem,) * 4,
-        name="tiled_order",
-    )(positions, polar.reshape(tiles, 128), field_ext, tile_atom.reshape(tiles, 128))
-
     sum_count = 2 * (inner + outer)
     ring_count = 1 + 2 * ITERS
-    x, r = pl.pallas_call(
+    x, r, slot = pl.pallas_call(
         functools.partial(solve_kernel, group, inner),
-        out_shape=(state, state),
-        in_specs=[vmem] * 3 + [smem] * 2,
-        out_specs=(vmem,) * 2,
+        out_shape=(state, state, shape(tiles, 128, dtype=jnp.int32)),
+        in_specs=[vmem] * 4 + [smem] * 2,
+        out_specs=(vmem,) * 3,
         scratch_shapes=[
+            pltpu.VMEM((tiles, 128), F32),
             pltpu.VMEM((tiles, steps, 6, ROWS, 128), F32),
             pltpu.VMEM((tiles, 2, steps, 6, ROWS, 128), F32),
             pltpu.VMEM((tiles, steps, 3, ROWS, 128), F32),
@@ -575,6 +590,7 @@
             pltpu.VMEM((ITERS, 3 * tiles, 128), F32),
             pltpu.VMEM((ITERS, 3 * tiles, 128), F32),
             pltpu.VMEM((6 * tiles, 128), F32),
+            pltpu.VMEM((3 * tiles, 128), F32),
             pltpu.VMEM((2 * tiles, 6 * tiles), jnp.bfloat16),
             pltpu.VMEM((128, 128), F32),
             pltpu.VMEM((128, 128), F32),
@@ -589,7 +605,14 @@
             collective_id=0, has_side_effects=True, vmem_limit_bytes=60 * 1024 * 1024
         ),
         name="solve",
-    )(pack, rhs, inv_alpha, tile_list, image_shift)
+    )(
+        positions,
+        polar.reshape(tiles, 128),
+        field_ext,
+        tile_atom.reshape(tiles, 128),
+        tile_list.T,
+        image_shift.transpose(2, 0, 1),
+    )
 
     return pl.pallas_call(
         atom_order_kernel,

time: 90.9 us -> 79.4 us (0.87)
  Pallas kernels: 87.8 us -> 78.4 us
  local copies, waits for them, and re-layouts: 2.07 us -> 0 us
    pallas_call x1, Pallas kernels: 82.8 us -> 76 us  [on_device(): pl.pallas_call(functools.partial(solve_kernel, group, inner), out_shape=(...]
    pallas_call x1 -> x0, Pallas kernels: 2.63 us -> none  [on_device(): pl.pallas_call(tiled_order_kernel, out_shape=(shape(4 * tiles, 128), shap...]
    unnamed x6 -> x0, local copies, waits for them, and re-layouts: 2.07 us -> none
where the time goes in v3:
time: 79.4 us; the launch traced here: 79 us
  Pallas kernels  78.4 us (99%)
    pallas_call x1, Pallas kernels, on_device(): pl.pallas_call(functools.partial(solve_kernel, group, inner), out_shape=(...  76 us
    pallas_call x1, Pallas kernels, on_device(): pl.pallas_call(atom_order_kernel, out_shape=(shape(3, atoms), shape(3, at...  2.38 us

profile of v3, /device:TPU:513, one launch (start us, length us, event | category | flops | bytes accessed | tf_op | source)
XLA Modules:
  0.0 79.0 jit_solution(15924611178354993327)
XLA Ops:
  0.6 76.0 %solve.1 = (f32[96,128]{1,0:T(8,128)}, f32[96,128]{1,0:T(8,128)}, s32[32,128]{1,0:T(8,128)}) custom-call(f32[3,4096]{1,0:T(4,128)} %pos_ref.1, f32[32,128]{1,0:T(8,128)} %bitcast.4, f32[3,4096]{1,0:T(4,128)} %field_ref.1, s32[32,128]{1,0:T(8,128)} %bitcast.5, s32[3,32]{1,0:T(4,128)} %bitcast.7, s32[3,2,32]{2,1,0:T(2,128)} %bitcast.6), custom_call_target="tpu_custom_call" | custom-call | tf_op jit(solution)/shard_map/solve/pallas_call | solution.py:573
  76.6 2.4 %atom_order.1 = (f32[3,4096]{1,0:T(4,128)}, f32[3,4096]{1,0:T(4,128)}) custom-call(f32[96,128]{1,0:T(8,128)} %get-tuple-element.5.x_ref, f32[96,128]{1,0:T(8,128)} %get-tuple-element.6.r_ref, s32[32,128]{1,0:T(8,128)} %get-tuple-element.7.slot_ref), custom_call_target="tpu_custom_call" | custom-call | tf_op jit(solution)/shard_map/atom_order/pallas_call | solution.py:617

commit v4 on v3

--- a/solution.py
+++ b/solution.py
@@ -1,4 +1,5 @@
 import functools
+import math
 
 import jax
 import jax.numpy as jnp
@@ -92,31 +93,19 @@
     inv = lax.rsqrt(square)
     minus_u = square * (square * inv) * (left[3] * right[3])
     decay = jnp.exp(minus_u)
-    inv_square = inv * inv
-    inv_cube = inv * inv_square
-    if diagonal is not None:
-        inv_cube = jnp.where(diagonal, 0.0, inv_cube)
+    inv_cube = inv * (inv * inv)
     rest = 1.0 - decay
     g3 = rest * inv_cube
-    g5 = (rest + minus_u * decay) * inv_cube * (3.0 * inv_square)
-    ax = g5 * dx
-    ay = g5 * dy
-    return (
-        ax * dx - g3,
-        ax * dy,
-        ax * dz,
-        ay * dy - g3,
-        ay * dz,
-        g5 * dz * dz - g3,
-    )
-
-
-def times(t, m):
-    return (
-        t[0] * m[0] + t[1] * m[1] + t[2] * m[2],
-        t[1] * m[0] + t[3] * m[1] + t[4] * m[2],
-        t[2] * m[0] + t[4] * m[1] + t[5] * m[2],
-    )
+    if diagonal is not None:
+        g3 = jnp.where(diagonal, 0.0, g3)
+    damped = (rest + minus_u * decay) * inv_cube
+    scale = (damped * lax.rsqrt(damped)) * (inv * math.sqrt(3.0))
+    return (dx * scale, dy * scale, dz * scale), g3
+
+
+def along(e, m):
+    share = e[0] * m[0] + e[1] * m[1] + e[2] * m[2]
+    return (e[0] * share, e[1] * share, e[2] * share)
 
 
 def solve_kernel(
@@ -147,6 +136,8 @@
     ret_in,
     right_rows,
     own_rows,
+    left_rows,
+    scalar_t,
     hot,
     colmat,
     gram,
@@ -263,22 +254,40 @@
         if vector is not None:
             lines = [lines[c] + vector[c] for c in range(3)] + lines[3:]
         lines[3] = lines[3] * (-THOLE)
-        return [jnp.broadcast_to(line, (ROWS, 128)) for line in lines]
-
-    block_sub = lax.broadcasted_iota(jnp.int32, (ROWS, 128), 0)
-    block_lane = lax.broadcasted_iota(jnp.int32, (ROWS, 128), 1)
+        return [jnp.broadcast_to(line, (2 * ROWS, 128)) for line in lines]
+
+    sub_16 = lax.broadcasted_iota(jnp.int32, (2 * ROWS, 128), 0)
+    lane_16 = lax.broadcasted_iota(jnp.int32, (2 * ROWS, 128), 1)
+    sub_8 = lax.broadcasted_iota(jnp.int32, (ROWS, 128), 0)
+    lines_of = [jnp.logical_or(sub_8 == c, sub_8 == c + 3) for c in range(3)]
+    halves = [jnp.logical_or(sub_16 == c, sub_16 == c + 3) for c in range(3)]
+
+    def tensors(t, cols, right, diagonal, where, place):
+        def block(i, carry):
+            left = [cols[pl.ds(2 * i, 2), c].reshape(2 * ROWS, 128) for c in range(4)]
+            same = sub_16 + i * (2 * ROWS) == lane_16 if diagonal else None
+            e, g3 = pair_tensor(left, right, same)
+            for c in range(3):
+                where(t, i, c, e[c].reshape(2, ROWS, 128))
+            high = g3.astype(jnp.bfloat16)
+            low = (g3 - high.astype(F32)).astype(jnp.bfloat16)
+            at = pl.multiple_of(i * (2 * ROWS), 2 * ROWS)
+            scalar_t[t, pl.ds(at, 2 * ROWS), lanes(place)] = high
+            scalar_t[t, pl.ds(128 + at, 2 * ROWS), lanes(place)] = low
+            return carry
+
+        lax.fori_loop(0, steps // 2, block, 0, unroll=True)
 
     def own_tensors(t, cols):
-        right = right_lines(t, None)
-
-        def block(i, carry):
-            left = [cols[i, c] for c in range(4)]
-            same = block_sub + i * ROWS == block_lane
-            for k, value in enumerate(pair_tensor(left, right, same)):
-                own_t[t, i, k] = value
-            return carry
-
-        lax.fori_loop(0, steps, block, 0, unroll=True)
+        def where(t, i, c, value):
+            own_t[t, pl.ds(2 * i, 2), c] = value
+
+        tensors(t, cols, right_lines(t, None), True, where, 2)
+
+    def split_lines(lines):
+        wide = jnp.where(halves[0], lines[0], jnp.where(halves[1], lines[1], lines[2]))
+        high = wide.astype(jnp.bfloat16).astype(F32)
+        return jnp.where(sub_16 < 3, high, wide - high).astype(jnp.bfloat16)
 
     last = me == group - 1
 
@@ -291,15 +300,11 @@
                 shift_ref[e + 1, 0, t].astype(F32) * 128.0,
                 shift_ref[e + 1, 1, t].astype(F32) * (2.0 * tiles),
             )
-            right = right_lines(n, vector)
-
-            def block(i, carry):
-                left = [cols[i, c] for c in range(4)]
-                for k, value in enumerate(pair_tensor(left, right, None)):
-                    pair_t[t, e, i, k] = value
-                return carry
-
-            lax.fori_loop(0, steps, block, 0, unroll=True)
+
+            def where(t, i, c, value, e=e):
+                pair_t[t, e, pl.ds(2 * i, 2), c] = value
+
+            tensors(t, cols, right_lines(n, vector), False, where, e)
 
     def in_pairs(ref, count, work, first=0, stop=tiles):
         spread(cols_a, ref, first, count)
@@ -322,8 +327,8 @@
             ]
 
             def block(i, inside):
-                tensor = [own_t[t, i, k] for k in range(6)]
-                for c, value in enumerate(times(tensor, m)):
+                tensor = [own_t[t, i, c] for c in range(3)]
+                for c, value in enumerate(along(tensor, m)):
                     part[t, i, c] = value
                 return inside
 
@@ -336,25 +341,32 @@
         sources = 3 if with_own else 2
 
         def work(t, cols):
+            lines = [
+                jnp.broadcast_to(win[pl.ds(c * tiles + t, 1), :], (2 * ROWS, 128))
+                for c in range(3)
+            ]
+            split = split_lines(lines)
+            scalar = jnp.dot(
+                jnp.concatenate([split, split], axis=1), scalar_t[t], preferred_element_type=F32
+            )[0:ROWS]
+
             def block(i, sums):
                 m = [cols[i, c] for c in range(3)]
                 new = []
                 for e in range(sources):
-                    tensor = [own_t[t, i, k] if e == 2 else pair_t[t, e, i, k] for k in range(6)]
-                    new += list(times(tensor, m))
+                    tensor = [own_t[t, i, c] if e == 2 else pair_t[t, e, i, c] for c in range(3)]
+                    new += list(along(tensor, m))
                 return tuple(a + b for a, b in zip(sums, new))
 
             zeros = (jnp.zeros((ROWS, 128), F32),) * (3 * sources)
             sums = lax.fori_loop(0, steps, block, zeros, unroll=True)
-            if with_own:
-                for c in range(3):
-                    own_rows[pl.ds(c * tiles + t, 1), :] = jnp.sum(
-                        sums[6 + c], axis=0, keepdims=True
-                    )
-            for e in range(2):
-                for c in range(3):
+            for c in range(3):
+                less = [jnp.where(lines_of[c], scalar[:, lanes(e)], 0.0) for e in range(3)]
+                own = sums[6 + c] - less[2] if with_own else -less[2]
+                own_rows[pl.ds(c * tiles + t, 1), :] = jnp.sum(own, axis=0, keepdims=True)
+                for e in range(2):
                     right_rows[pl.ds(2 * tiles * c + 2 * t + e, 1), :] = jnp.sum(
-                        sums[3 * e + c], axis=0, keepdims=True
+                        sums[3 * e + c] - less[e], axis=0, keepdims=True
                     )
 
         in_pairs(win, 3, work)
@@ -391,16 +403,28 @@
                 first = n + jnp.where(n >= tiles, 2 * tiles, 0)
                 m.append(
                     [
-                        jnp.broadcast_to(win[pl.ds(first + c * tiles, 1), :], (ROWS, 128))
+                        jnp.broadcast_to(win[pl.ds(first + c * tiles, 1), :], (2 * ROWS, 128))
                         for c in range(3)
                     ]
                 )
+            scalar = lax.dot_general(
+                jnp.concatenate([split_lines(lines) for lines in m], axis=1),
+                scalar_t[t, :, 0:256],
+                (((1,), (1,)), ((), ())),
+                preferred_element_type=F32,
+            )[0:ROWS]
+            scalar = scalar[:, lanes(0)] + scalar[:, lanes(1)]
+            for c in range(3):
+                left_rows[pl.ds(c * tiles + t, 1), :] = jnp.sum(
+                    jnp.where(lines_of[c], scalar, 0.0), axis=0, keepdims=True
+                )
+            m = [[line[0:ROWS] for line in lines] for lines in m]
 
             def block(i, inside):
                 sums = [part[t, i, c] for c in range(3)] if with_part else None
                 for e in range(2):
-                    tensor = [pair_t[t, e, i, k] for k in range(6)]
-                    new = times(tensor, m[e])
+                    tensor = [pair_t[t, e, i, c] for c in range(3)]
+                    new = along(tensor, m[e])
                     sums = new if sums is None else [a + b for a, b in zip(sums, new)]
                 for c in range(3):
                     part[t, i, c] = sums[c]
@@ -415,7 +439,7 @@
 
         lax.fori_loop(0, tiles // 4, body, 0)
         gather_column(tiles - 1)
-        return colmat[...].T[0 : 3 * tiles]
+        return colmat[...].T[0 : 3 * tiles] - left_rows[...]
 
     in_pairs(win_p, 4, own_tensors, 0, tiles // 2)
 
@@ -477,7 +501,7 @@
         if final:
             now = own_vector(k)
             line = inner_rows(now, shifted * now - (own_rows[...] + 2.0 * kept))
-            kept = kept + own_rows[...]
+        kept = kept + own_rows[...]
         returns[k].start()
         if k > 0 and not final:
             own_fields(wins[k], 4, tiles)
@@ -577,8 +601,8 @@
         out_specs=(vmem,) * 3,
         scratch_shapes=[
             pltpu.VMEM((tiles, 128), F32),
-            pltpu.VMEM((tiles, steps, 6, ROWS, 128), F32),
-            pltpu.VMEM((tiles, 2, steps, 6, ROWS, 128), F32),
+            pltpu.VMEM((tiles, steps, 3, ROWS, 128), F32),
+            pltpu.VMEM((tiles, 2, steps, 3, ROWS, 128), F32),
             pltpu.VMEM((tiles, steps, 3, ROWS, 128), F32),
             pltpu.VMEM((steps, 4, ROWS, 128), F32),
             pltpu.VMEM((steps, 4, ROWS, 128), F32),
@@ -591,6 +615,8 @@
             pltpu.VMEM((ITERS, 3 * tiles, 128), F32),
             pltpu.VMEM((6 * tiles, 128), F32),
             pltpu.VMEM((3 * tiles, 128), F32),
+            pltpu.VMEM((3 * tiles, 128), F32),
+            pltpu.VMEM((tiles, 256, 384), jnp.bfloat16),
             pltpu.VMEM((2 * tiles, 6 * tiles), jnp.bfloat16),
             pltpu.VMEM((128, 128), F32),
             pltpu.VMEM((128, 128), F32),

time: 79.4 us -> 73.4 us (0.924)
  Pallas kernels: 78.4 us -> 72.5 us
    pallas_call x1, Pallas kernels: 76 us -> 70.2 us  [on_device(): pl.pallas_call(functools.partial(solve_kernel, group, inner), out_shape=(...]
where the time goes in v4:
time: 73.4 us; the launch traced here: 73.2 us
  Pallas kernels  72.5 us (99%)
    pallas_call x1, Pallas kernels, on_device(): pl.pallas_call(functools.partial(solve_kernel, group, inner), out_shape=(...  70.2 us
    pallas_call x1, Pallas kernels, on_device(): pl.pallas_call(atom_order_kernel, out_shape=(shape(3, atoms), shape(3, at...  2.38 us

profile of v4, /device:TPU:513, one launch (start us, length us, event | category | flops | bytes accessed | tf_op | source)
XLA Modules:
  0.0 73.2 jit_solution(4215816710177401675)
XLA Ops:
  0.6 70.2 %solve.1 = (f32[96,128]{1,0:T(8,128)}, f32[96,128]{1,0:T(8,128)}, s32[32,128]{1,0:T(8,128)}) custom-call(f32[3,4096]{1,0:T(4,128)} %pos_ref.1, f32[32,128]{1,0:T(8,128)} %bitcast.4, f32[3,4096]{1,0:T(4,128)} %field_ref.1, s32[32,128]{1,0:T(8,128)} %bitcast.5, s32[3,32]{1,0:T(4,128)} %bitcast.7, s32[3,2,32]{2,1,0:T(2,128)} %bitcast.6), custom_call_target="tpu_custom_call" | custom-call | tf_op jit(solution)/shard_map/solve/pallas_call | solution.py:597
  70.8 2.4 %atom_order.1 = (f32[3,4096]{1,0:T(4,128)}, f32[3,4096]{1,0:T(4,128)}) custom-call(f32[96,128]{1,0:T(8,128)} %get-tuple-element.5.x_ref, f32[96,128]{1,0:T(8,128)} %get-tuple-element.6.r_ref, s32[32,128]{1,0:T(8,128)} %get-tuple-element.7.slot_ref), custom_call_target="tpu_custom_call" | custom-call | tf_op jit(solution)/shard_map/atom_order/pallas_call | solution.py:643

commit v5 on v4

--- a/solution.py
+++ b/solution.py
@@ -126,6 +126,8 @@
     part,
     cols_a,
     cols_b,
+    cols_c,
+    cols_d,
     win_p,
     win_0,
     win_1,
@@ -157,6 +159,7 @@
     peers_1 = [row * inner + lax.rem(col + d, inner) for d in range(1, inner)]
     peers_2 = [lax.rem(row + d, outer) * inner + col for d in range(1, outer)]
     wins = (win_0, win_1, win_2, win_3)
+    cols = (cols_a, cols_b, cols_c, cols_d)
 
     barrier = pltpu.get_barrier_semaphore()
     everyone = [after, before] + peers_1 + peers_2
@@ -218,28 +221,23 @@
     def unpacked(sums):
         gram[...] = jnp.broadcast_to(sums, (128, 128)).T
 
-    def rows_at(step):
-        places = pl.ds(pl.multiple_of(step * 128, 128), 128)
-        rows = [pos_ref[c : c + 1, places] for c in range(3)]
-        rows += [field_ref[c : c + 1, places] for c in range(3)]
-        return rows + [polar_ref[pl.ds(step, 1), :]]
-
-    for block, found in enumerate(gathered(atom_ref[...], rows_at, 7, tiles)):
+    def rows_at(ref):
+        def rows(step):
+            places = pl.ds(pl.multiple_of(step * 128, 128), 128)
+            return [ref[c : c + 1, places] for c in range(3)]
+
+        return rows
+
+    def place_rows(step):
+        return rows_at(pos_ref)(step) + [polar_ref[pl.ds(step, 1), :]]
+
+    for block, found in enumerate(gathered(atom_ref[...], place_rows, 4, tiles)):
         for c in range(3):
             at = c * tiles + 8 * block
             win_p[at : at + 8, :] = found[c]
-            win_0[at : at + 8, :] = found[3 + c]
         at = 3 * tiles + 8 * block
-        win_p[at : at + 8, :] = lax.rsqrt(found[6])
-        inv_alpha_ref[8 * block : 8 * block + 8, :] = 1.0 / found[6]
-
-    rhs = win_0[0 : 3 * tiles, :]
-    inv_alpha = inv_alpha_ref[...]
-    inv_alpha_3 = jnp.concatenate([inv_alpha] * 3, axis=0)
-    colmat[...] = jnp.zeros((128, 128), F32)
-    gram[...] = jnp.zeros((128, 128), F32)
-    gram[0:1, :] = inner_rows(rhs, rhs)
-    gram[1:2, :] = inner_rows(rhs, rhs * inv_alpha_3)
+        win_p[at : at + 8, :] = lax.rsqrt(found[3])
+        inv_alpha_ref[8 * block : 8 * block + 8, :] = 1.0 / found[3]
 
     steps = 128 // ROWS
 
@@ -307,14 +305,14 @@
             tensors(t, cols, right_lines(n, vector), False, where, e)
 
     def in_pairs(ref, count, work, first=0, stop=tiles):
-        spread(cols_a, ref, first, count)
+        spread(cols[0], ref, first, count)
 
         def body(u, carry):
             t = first + 2 * u
-            spread(cols_b, ref, t + 1, count)
-            work(t, cols_a)
-            spread(cols_a, ref, lax.rem(t + 2, tiles), count)
-            work(t + 1, cols_b)
+            spread(cols[1], ref, t + 1, count)
+            work(t, cols[0])
+            spread(cols[0], ref, lax.rem(t + 2, tiles), count)
+            work(t + 1, cols[1])
             return carry
 
         lax.fori_loop(0, (stop - first) // 2, body, 0)
@@ -336,6 +334,21 @@
             return carry
 
         lax.fori_loop(first, stop, body, 0)
+
+    def in_fours(ref, count, work):
+        for slot, buf in enumerate(cols[0:2]):
+            spread(buf, ref, slot, count)
+
+        def body(u, carry):
+            t = 4 * u
+            for half in range(2):
+                for step in range(2):
+                    ahead = lax.rem(t + 2 * half + 2 + step, tiles)
+                    spread(cols[2 * (1 - half) + step], ref, ahead, count)
+                    work(t + 2 * half + step, cols[2 * half + step])
+            return carry
+
+        lax.fori_loop(0, tiles // 4, body, 0)
 
     def right_fields(win, with_own):
         sources = 3 if with_own else 2
@@ -369,7 +382,7 @@
                         sums[3 * e + c] - less[e], axis=0, keepdims=True
                     )
 
-        in_pairs(win, 3, work)
+        in_fours(win, 3, work)
         rows = right_rows[...]
         rows = jnp.concatenate(
             [rows[2 * tiles * c : 2 * tiles * (c + 1)] for c in range(3)], axis=1
@@ -433,11 +446,11 @@
             lax.fori_loop(0, steps, block, 0, unroll=True)
 
         def body(u, carry):
-            for step in range(4):
-                one(4 * u + step)
+            for step in range(8):
+                one(8 * u + step)
             return carry
 
-        lax.fori_loop(0, tiles // 4, body, 0)
+        lax.fori_loop(0, tiles // 8, body, 0)
         gather_column(tiles - 1)
         return colmat[...].T[0 : 3 * tiles] - left_rows[...]
 
@@ -447,6 +460,20 @@
     own_p, own_v = 4 * tiles, 3 * tiles
     halo_p = ring_copy(win_p.at[0:own_p], win_p.at[own_p : 2 * own_p], 0, before)
     halo_p.start()
+
+    for block, found in enumerate(gathered(atom_ref[...], rows_at(field_ref), 3, tiles)):
+        for c in range(3):
+            at = c * tiles + 8 * block
+            win_0[at : at + 8, :] = found[c]
+
+    rhs = win_0[0 : 3 * tiles, :]
+    inv_alpha = inv_alpha_ref[...]
+    inv_alpha_3 = jnp.concatenate([inv_alpha] * 3, axis=0)
+    colmat[...] = jnp.zeros((128, 128), F32)
+    gram[...] = jnp.zeros((128, 128), F32)
+    gram[0:1, :] = inner_rows(rhs, rhs)
+    gram[1:2, :] = inner_rows(rhs, rhs * inv_alpha_3)
+
     halos = [
         ring_copy(win.at[0:own_v], win.at[own_v : 2 * own_v], 1 + k, before)
         for k, win in enumerate(wins)
@@ -587,7 +614,6 @@
     steps = 128 // ROWS
     vmem = pl.BlockSpec(memory_space=pltpu.VMEM)
     smem = pl.BlockSpec(memory_space=pltpu.SMEM)
-    state = jax.ShapeDtypeStruct((3 * tiles, 128), F32)
 
     def shape(*dims, dtype=F32):
         return jax.ShapeDtypeStruct(dims, dtype)
@@ -596,7 +622,11 @@
     ring_count = 1 + 2 * ITERS
     x, r, slot = pl.pallas_call(
         functools.partial(solve_kernel, group, inner),
-        out_shape=(state, state, shape(tiles, 128, dtype=jnp.int32)),
+        out_shape=(
+            pltpu.VMEM((3 * tiles, 128), F32),
+            pltpu.VMEM((3 * tiles, 128), F32),
+            pltpu.VMEM((tiles, 128), jnp.int32),
+        ),
         in_specs=[vmem] * 4 + [smem] * 2,
         out_specs=(vmem,) * 3,
         scratch_shapes=[
@@ -606,6 +636,8 @@
             pltpu.VMEM((tiles, steps, 3, ROWS, 128), F32),
             pltpu.VMEM((steps, 4, ROWS, 128), F32),
             pltpu.VMEM((steps, 4, ROWS, 128), F32),
+            pltpu.VMEM((steps, 3, ROWS, 128), F32),
+            pltpu.VMEM((steps, 3, ROWS, 128), F32),
             pltpu.VMEM((8 * tiles, 128), F32),
         ]
         + [pltpu.VMEM((6 * tiles, 128), F32)] * ITERS
@@ -646,7 +678,7 @@
         in_specs=[vmem] * 3,
         out_specs=(vmem,) * 2,
         name="atom_order",
-    )(x, r, slot)
+    )(*(pltpu.with_memory_space_constraint(value, pltpu.VMEM) for value in (x, r, slot)))
 
 
 def solution(mesh):

time: 73.4 us -> 71.2 us (0.970)
  Pallas kernels: 72.5 us -> 70.4 us
    pallas_call x1, Pallas kernels: 70.2 us -> 68.8 us  [on_device(): pl.pallas_call(functools.partial(solve_kernel, group, inner), out_shape=(...]
    pallas_call x1, Pallas kernels: 2.38 us -> 1.56 us  [on_device(): pl.pallas_call(atom_order_kernel, out_shape=(shape(3, atoms), shape(3, at...]
where the time goes in v5:
time: 71.2 us; the launch traced here: 71 us
  Pallas kernels  70.4 us (99%)
    pallas_call x1, Pallas kernels, on_device(): pl.pallas_call(functools.partial(solve_kernel, group, inner), out_shape=(...  68.8 us
    pallas_call x1, Pallas kernels, on_device(): pl.pallas_call(atom_order_kernel, out_shape=(shape(3, atoms), shape(3, at...  1.56 us

profile of v5, /device:TPU:513, one launch (start us, length us, event | category | flops | bytes accessed | tf_op | source)
XLA Modules:
  0.0 71.0 jit_solution(5701508647351710485)
XLA Ops:
  0.6 68.8 %solve.1 = (f32[96,128]{1,0:T(8,128)S(1)}, f32[96,128]{1,0:T(8,128)S(1)}, s32[32,128]{1,0:T(8,128)S(1)}) custom-call(f32[3,4096]{1,0:T(4,128)} %pos_ref.1, f32[32,128]{1,0:T(8,128)} %bitcast.4, f32[3,4096]{1,0:T(4,128)} %field_ref.1, s32[32,128]{1,0:T(8,128)} %bitcast.5, s32[3,32]{1,0:T(4,128)} %bitcast.7, s32[3,2,32]{2,1,0:T(2,128)} %bitcast.6), custom_call_target="tpu_custom_call" | custom-call | tf_op jit(solution)/shard_map/solve/pallas_call | solution.py:623
  69.5 1.6 %atom_order.1 = (f32[3,4096]{1,0:T(4,128)}, f32[3,4096]{1,0:T(4,128)}) custom-call(f32[96,128]{1,0:T(8,128)S(1)} %get-tuple-element.5.x_ref, f32[96,128]{1,0:T(8,128)S(1)} %get-tuple-element.6.r_ref, s32[32,128]{1,0:T(8,128)S(1)} %get-tuple-element.7.slot_ref), custom_call_target="tpu_custom_call" | custom-call | tf_op jit(solution)/shard_map/atom_order/pallas_call | solution.py:675

commit v6 on v5

--- a/solution.py
+++ b/solution.py
@@ -117,6 +117,7 @@
     atom_ref,
     list_ref,
     shift_ref,
+    lines_ref,
     x_ref,
     r_ref,
     slot_ref,
@@ -378,7 +379,7 @@
                 own = sums[6 + c] - less[2] if with_own else -less[2]
                 own_rows[pl.ds(c * tiles + t, 1), :] = jnp.sum(own, axis=0, keepdims=True)
                 for e in range(2):
-                    right_rows[pl.ds(2 * tiles * c + 2 * t + e, 1), :] = jnp.sum(
+                    right_rows[pl.ds(tiles * (2 * c + e) + t, 1), :] = jnp.sum(
                         sums[3 * e + c] - less[e], axis=0, keepdims=True
                     )
 
@@ -454,7 +455,7 @@
         gather_column(tiles - 1)
         return colmat[...].T[0 : 3 * tiles] - left_rows[...]
 
-    in_pairs(win_p, 4, own_tensors, 0, tiles // 2)
+    in_pairs(win_p, 4, own_tensors, 0, tiles // 4)
 
     pl.semaphore_wait(barrier, len(everyone))
     own_p, own_v = 4 * tiles, 3 * tiles
@@ -484,22 +485,12 @@
     halos[0].start()
     sum_start(0, 0, packed_sums(gram[0:16, :]))
 
-    in_pairs(win_p, 4, own_tensors, tiles // 2, tiles)
+    in_pairs(win_p, 4, own_tensors, tiles // 4, tiles)
     own_fields(win_0)
 
-    hot_lane = lax.broadcasted_iota(jnp.int32, (1, 128), 1)
-
-    def mark(t, carry):
-        for e in range(2):
-            value = jnp.where(hot_lane == list_ref[e + 1, t], 1.0, 0.0)
-            gram[pl.ds(2 * t + e, 1), :] = value
-        return carry
-
-    lax.fori_loop(0, tiles, mark, 0)
-    marks = gram[...].T[0 : 2 * tiles, 0 : 2 * tiles].astype(jnp.bfloat16)
-    hot[...] = jnp.concatenate([marks] * 3, axis=1)
-    gram[...] = jnp.zeros((128, 128), F32)
-    slot_ref[...] = inverse_order(atom_ref[...])
+    tile_ids = lax.broadcasted_iota(jnp.int32, (2 * tiles, tiles), 0)
+    marks = [jnp.where(lines_ref[e : e + 1, :] == tile_ids, 1.0, 0.0) for e in (1, 2)]
+    hot[...] = jnp.concatenate(marks * 3, axis=1).astype(jnp.bfloat16)
 
     halo_p.wait()
     in_pairs(win_p, 4, pair_tensors)
@@ -518,9 +509,10 @@
     for k in range(ITERS):
         final = k + 1 == ITERS
         if k > 0:
-            for j in range(k + 1):
+            keep((k, k), inner_rows(own_vector(k), own_vector(k)))
+            halos[k].start()
+            for j in range(k):
                 keep((j, k), inner_rows(own_vector(j), own_vector(k)))
-            halos[k].start()
         kept, sent = right_fields(wins[k], final)
         ret_out[k] = sent
         if k > 0 and not final:
@@ -545,6 +537,7 @@
             keep((0, 0), inner_rows(rhs, rhs))
             shifted = jnp.concatenate([inv_alpha - centre] * 3, axis=0)
         if final:
+            slot_ref[...] = inverse_order(atom_ref[...])
             sum_start(1, 1, sum_finish(1, 0))
         returns[k].wait()
         new = shifted * own_vector(k) - (field + ret_in[k])
@@ -563,12 +556,10 @@
         return gram[index : index + 1, :]
 
     def form(a, b):
-        out = None
-        for i, p in enumerate(a):
-            for j, q in enumerate(b):
-                term = p * q * entry(i, j)
-                out = term if out is None else out + term
-        return out
+        terms = [p * (q * entry(i, j)) for i, p in enumerate(a) for j, q in enumerate(b)]
+        while len(terms) > 1:
+            terms = [sum(terms[i + 1 : i + 2], terms[i]) for i in range(0, len(terms), 2)]
+        return terms[0]
 
     def plus(a, scale, b):
         out = []
@@ -627,7 +618,7 @@
             pltpu.VMEM((3 * tiles, 128), F32),
             pltpu.VMEM((tiles, 128), jnp.int32),
         ),
-        in_specs=[vmem] * 4 + [smem] * 2,
+        in_specs=[vmem] * 4 + [smem] * 2 + [vmem],
         out_specs=(vmem,) * 3,
         scratch_shapes=[
             pltpu.VMEM((tiles, 128), F32),
@@ -670,6 +661,7 @@
         tile_atom.reshape(tiles, 128),
         tile_list.T,
         image_shift.transpose(2, 0, 1),
+        tile_list.T,
     )
 
     return pl.pallas_call(

time: 71.2 us -> 71.1 us (level)
  no operation moved by 1% of the time
where the time goes in v6:
time: 71.1 us; the launch traced here: 71 us
  Pallas kernels  70.4 us (99%)
    pallas_call x1, Pallas kernels, on_device(): pl.pallas_call(functools.partial(solve_kernel, group, inner), out_shape=(...  68.8 us
    pallas_call x1, Pallas kernels, on_device(): pl.pallas_call(atom_order_kernel, out_shape=(shape(3, atoms), shape(3, at...  1.56 us

profile of v6, /device:TPU:513, one launch (start us, length us, event | category | flops | bytes accessed | tf_op | source)
XLA Modules:
  0.0 71.0 jit_solution(16509513702465783610)
XLA Ops:
  0.6 68.8 %solve.1 = (f32[96,128]{1,0:T(8,128)S(1)}, f32[96,128]{1,0:T(8,128)S(1)}, s32[32,128]{1,0:T(8,128)S(1)}) custom-call(f32[3,4096]{1,0:T(4,128)} %pos_ref.1, f32[32,128]{1,0:T(8,128)} %bitcast.4, f32[3,4096]{1,0:T(4,128)} %field_ref.1, s32[32,128]{1,0:T(8,128)} %bitcast.5, s32[3,32]{1,0:T(4,128)} %bitcast.6, s32[3,2,32]{2,1,0:T(2,128)} %bitcast.8, s32[3,32]{1,0:T(4,128)} %bitcast.7), custom_call_target="tpu_custom_call" | custom-call | tf_op jit(solution)/shard_map/solve/pallas_call | solution.py:614
  69.4 1.6 %atom_order.1 = (f32[3,4096]{1,0:T(4,128)}, f32[3,4096]{1,0:T(4,128)}) custom-call(f32[96,128]{1,0:T(8,128)S(1)} %get-tuple-element.5.x_ref, f32[96,128]{1,0:T(8,128)S(1)} %get-tuple-element.6.r_ref, s32[32,128]{1,0:T(8,128)S(1)} %get-tuple-element.7.slot_ref), custom_call_target="tpu_custom_call" | custom-call | tf_op jit(solution)/shard_map/atom_order/pallas_call | solution.py:667

commit v7 on v6

--- a/solution.py
+++ b/solution.py
@@ -305,19 +305,6 @@
 
             tensors(t, cols, right_lines(n, vector), False, where, e)
 
-    def in_pairs(ref, count, work, first=0, stop=tiles):
-        spread(cols[0], ref, first, count)
-
-        def body(u, carry):
-            t = first + 2 * u
-            spread(cols[1], ref, t + 1, count)
-            work(t, cols[0])
-            spread(cols[0], ref, lax.rem(t + 2, tiles), count)
-            work(t + 1, cols[1])
-            return carry
-
-        lax.fori_loop(0, (stop - first) // 2, body, 0)
-
     def own_fields(win, first=0, stop=tiles):
         def body(t, carry):
             m = [
@@ -336,20 +323,21 @@
 
         lax.fori_loop(first, stop, body, 0)
 
-    def in_fours(ref, count, work):
+    def in_turns(ref, count, work, turns, first=0, stop=tiles):
         for slot, buf in enumerate(cols[0:2]):
-            spread(buf, ref, slot, count)
+            spread(buf, ref, first + slot, count)
 
         def body(u, carry):
-            t = 4 * u
-            for half in range(2):
+            t = first + 2 * turns * u
+            for turn in range(turns):
+                now, later = 2 * (turn % 2), 2 * ((turn + 1) % 2)
                 for step in range(2):
-                    ahead = lax.rem(t + 2 * half + 2 + step, tiles)
-                    spread(cols[2 * (1 - half) + step], ref, ahead, count)
-                    work(t + 2 * half + step, cols[2 * half + step])
+                    ahead = lax.rem(t + 2 * turn + 2 + step, tiles)
+                    spread(cols[later + step], ref, ahead, count)
+                    work(t + 2 * turn + step, cols[now + step])
             return carry
 
-        lax.fori_loop(0, tiles // 4, body, 0)
+        lax.fori_loop(0, (stop - first) // (2 * turns), body, 0)
 
     def right_fields(win, with_own):
         sources = 3 if with_own else 2
@@ -383,7 +371,7 @@
                         sums[3 * e + c] - less[e], axis=0, keepdims=True
                     )
 
-        in_fours(win, 3, work)
+        in_turns(win, 3, work, 4)
         rows = right_rows[...]
         rows = jnp.concatenate(
             [rows[2 * tiles * c : 2 * tiles * (c + 1)] for c in range(3)], axis=1
@@ -455,7 +443,7 @@
         gather_column(tiles - 1)
         return colmat[...].T[0 : 3 * tiles] - left_rows[...]
 
-    in_pairs(win_p, 4, own_tensors, 0, tiles // 4)
+    in_turns(win_p, 4, own_tensors, 2, 0, tiles // 4)
 
     pl.semaphore_wait(barrier, len(everyone))
     own_p, own_v = 4 * tiles, 3 * tiles
@@ -485,7 +473,7 @@
     halos[0].start()
     sum_start(0, 0, packed_sums(gram[0:16, :]))
 
-    in_pairs(win_p, 4, own_tensors, tiles // 4, tiles)
+    in_turns(win_p, 4, own_tensors, 4, tiles // 4, tiles)
     own_fields(win_0)
 
     tile_ids = lax.broadcasted_iota(jnp.int32, (2 * tiles, tiles), 0)
@@ -493,7 +481,7 @@
     hot[...] = jnp.concatenate(marks * 3, axis=1).astype(jnp.bfloat16)
 
     halo_p.wait()
-    in_pairs(win_p, 4, pair_tensors)
+    in_turns(win_p, 4, pair_tensors, 2)
     sum_start(0, 1, sum_finish(0, 0))
 
     def own_vector(k):
@@ -627,8 +615,8 @@
             pltpu.VMEM((tiles, steps, 3, ROWS, 128), F32),
             pltpu.VMEM((steps, 4, ROWS, 128), F32),
             pltpu.VMEM((steps, 4, ROWS, 128), F32),
-            pltpu.VMEM((steps, 3, ROWS, 128), F32),
-            pltpu.VMEM((steps, 3, ROWS, 128), F32),
+            pltpu.VMEM((steps, 4, ROWS, 128), F32),
+            pltpu.VMEM((steps, 4, ROWS, 128), F32),
             pltpu.VMEM((8 * tiles, 128), F32),
         ]
         + [pltpu.VMEM((6 * tiles, 128), F32)] * ITERS

time: 71.1 us -> 69.9 us (0.983)
  Pallas kernels: 70.4 us -> 69.1 us
    pallas_call x1, Pallas kernels: 68.8 us -> 67.5 us  [on_device(): pl.pallas_call(functools.partial(solve_kernel, group, inner), out_shape=(...]
where the time goes in v7:
time: 69.9 us; the launch traced here: 69.7 us
  Pallas kernels  69.1 us (99%)
    pallas_call x1, Pallas kernels, on_device(): pl.pallas_call(functools.partial(solve_kernel, group, inner), out_shape=(...  67.5 us
    pallas_call x1, Pallas kernels, on_device(): pl.pallas_call(atom_order_kernel, out_shape=(shape(3, atoms), shape(3, at...  1.56 us

profile of v7, /device:TPU:513, one launch (start us, length us, event | category | flops | bytes accessed | tf_op | source)
XLA Modules:
  0.0 69.7 jit_solution(15165219653859043735)
XLA Ops:
  0.6 67.5 %solve.1 = (f32[96,128]{1,0:T(8,128)S(1)}, f32[96,128]{1,0:T(8,128)S(1)}, s32[32,128]{1,0:T(8,128)S(1)}) custom-call(f32[3,4096]{1,0:T(4,128)} %pos_ref.1, f32[32,128]{1,0:T(8,128)} %bitcast.4, f32[3,4096]{1,0:T(4,128)} %field_ref.1, s32[32,128]{1,0:T(8,128)} %bitcast.5, s32[3,32]{1,0:T(4,128)} %bitcast.6, s32[3,2,32]{2,1,0:T(2,128)} %bitcast.8, s32[3,32]{1,0:T(4,128)} %bitcast.7), custom_call_target="tpu_custom_call" | custom-call | tf_op jit(solution)/shard_map/solve/pallas_call | solution.py:602
  68.2 1.6 %atom_order.1 = (f32[3,4096]{1,0:T(4,128)}, f32[3,4096]{1,0:T(4,128)}) custom-call(f32[96,128]{1,0:T(8,128)S(1)} %get-tuple-element.5.x_ref, f32[96,128]{1,0:T(8,128)S(1)} %get-tuple-element.6.r_ref, s32[32,128]{1,0:T(8,128)S(1)} %get-tuple-element.7.slot_ref), custom_call_target="tpu_custom_call" | custom-call | tf_op jit(solution)/shard_map/atom_order/pallas_call | solution.py:655
